TPU v7x, 1024 devices: a whole 8x8x8 slice. The times are simulated.
1024 devices in a mesh: lat: 64 (over x, y), lev: 16 (over z, core).
Axes of the slice: x: 8, y: 8, z: 8, core: 2. Of those that a mesh axis runs over, the one named last changes fastest.
Arguments:
- fourier: bfloat16 [256, 2560, 128], P('lev', 'lat'), may hold values from -6 to 6
- quad_weights: float32 [2560], P('lat'), may hold values from 0.005 to 0.05
- legendre: bfloat16 [2560, 64, 1280], P('lat'), may hold values from -6 to 6
- owner_pair: int32 [64], replicated, may hold values from 0 to 63, each once
Outputs:
- spectra: float32 [64, 256, 1280], P('lat', 'lev')
- energy: float32 [], replicated
Inputs may be any that keep to these rules, and one draw needn't show every extreme that they name: `owner_pair`: a permutation of 0 to 63.
All inputs are finite; a program needn't handle non-finite values.
Results may differ from a plain program's by a relative error of at most 0.00094.
Values may be sent and summed in bfloat16 or wider, within the bound.
A program may use at most 64 MiB of HBM per device.

v0:
```python
import functools

import jax
import jax.numpy as jnp
from jax import lax
from jax.sharding import Mesh
from jax.sharding import PartitionSpec as P

TRUNC = 1280
M_WIN = 128
SPACING = 10
LAT = ("lat_0", "lat_1")
LEV = ("lev_0", "lev_1")
LAT_LEV = ("lat_0", "lat_1", "lev_0", "lev_1")


def sent_together(arrays, axis, split_dim, concat_dim, along):
    columns = [a.reshape(*a.shape[:along], -1) for a in arrays]
    both = jnp.concatenate(columns, axis=along)
    result, at, done = (
        lax.all_to_all(both, axis, split_axis=split_dim, concat_axis=concat_dim, tiled=True),
        0,
        [],
    )
    for a, column in zip(arrays, columns):
        section = result[..., at : at + column.shape[along]]
        done.append(section.reshape(*section.shape[:along], *a.shape[along:]))
        at += column.shape[along]
    return tuple(done)


def copy_for_each(value, axis):
    length = lax.axis_size(axis)
    return lax.all_to_all(
        jnp.broadcast_to(value[None], (length, *value.shape)), axis, 0, 0, tiled=True
    )


def laid_out(parts, dim):
    lengths = list(parts.shape[1:])
    lengths[dim] *= parts.shape[0]
    return jnp.moveaxis(parts, 0, dim).reshape(lengths)


def gathered_copies(value, axis, dim):
    parts = copy_for_each(value, axis)
    return laid_out(parts, dim)


def by_axis(value, axes):
    return functools.reduce(lax.psum, axes, value)


def shards(fourier, quad_weights, legendre, owner_pair):
    weighted = (fourier.astype(jnp.float32) * quad_weights[None, :, None]).astype(jnp.bfloat16)
    ch_dev = fourier.shape[0]
    pair_total = legendre.shape[1]
    pair_len = legendre.shape[2]
    owned = pair_total // lax.axis_size(LAT)
    lev_index = lax.axis_index(LEV)
    slice_len = pair_len // lax.axis_size(LEV)
    first_column = lev_index * slice_len
    column_block = lax.dynamic_slice_in_dim(legendre, first_column, slice_len, 2)
    legendre_part = jnp.take(column_block, owner_pair, axis=1)
    low_wave = jnp.take(weighted, owner_pair, axis=2)
    high_wave = jnp.take(weighted, M_WIN - 1 - owner_pair, axis=2)
    wave_rows = jnp.stack([low_wave, high_wave], 0).transpose(2, 3, 0, 1)
    gathered_table, gathered_waves = sent_together((legendre_part, wave_rows), LAT, 1, 0, 2)
    pair_ids = lax.dynamic_slice_in_dim(owner_pair, lax.axis_index(LAT) * owned, owned)
    column_ids = first_column + jnp.arange(slice_len, dtype=jnp.int32)
    low_limit = TRUNC - SPACING * pair_ids - SPACING // 2
    low_mask = column_ids[None, None, :] < low_limit[:, None, None]
    slab_rows = gathered_copies(gathered_waves, LEV, 3)
    low_part = jnp.einsum(
        "lpc,lpk->pck", slab_rows[:, :, 0, :], gathered_table, preferred_element_type=jnp.float32
    )
    high_part = jnp.einsum(
        "lpc,lpk->pck", slab_rows[:, :, 1, :], gathered_table, preferred_element_type=jnp.float32
    )
    all_channels = jnp.where(low_mask, low_part, high_part)
    spectra = lax.all_to_all(all_channels, LEV, split_axis=1, concat_axis=2, tiled=True)
    levels = ch_dev * lax.axis_size(LEV) // 2
    channel_ids = lev_index * ch_dev + jnp.arange(ch_dev, dtype=jnp.int32)
    level_factor = 1.0 + 2.0 * (channel_ids // 2).astype(jnp.float32) / (levels - 1)
    local_sum = jnp.sum(level_factor[None, :, None] * spectra * spectra)
    energy = by_axis(local_sum, LAT_LEV) / (pair_total * 2 * levels * pair_len)
    return (spectra, energy)


def solution(mesh):
    finer = Mesh(mesh.devices.reshape(8, 8, 8, 2), ("lat_0", "lat_1", "lev_0", "lev_1"))
    return jax.shard_map(
        shards,
        mesh=finer,
        in_specs=(P(LEV, LAT, None), P(LAT), P(LAT, None, None), P()),
        out_specs=(P(LAT, LEV, None), P()),
        check_vma=False,
    )
```

profile of v0, /device:TPU:1, one launch (start us, length us, event | category | flops | bytes accessed | tf_op | source)
XLA Modules:
  0.0 194.8 jit_solution(4946511651595859847)
XLA Ops:
  0.6 0.7 compare_select_fusion.1
  1.3 0.7 compare_and_fusion.2
  2.0 1.0 multiply_convert_fusion
  3.4 0.6 gather_fusion.2
  4.1 0.6 gather_fusion.1
  5.1 0.7 copy.41
  6.2 1.6 constant_dynamic-slice_fusion
  8.2 0.7 gather_fusion
  9.5 29.6 %all_to_all.41 = bf16[40,64,112]{2,0,1:T(8,128)(2,1)S(1)} all-to-all(bf16[40,64,112]{2,0,1:T(8,128)(2,1)S(1)} %pad_maximum_fusion), channel_id=1, replica_groups=mesh['lat_0'=8,'lat_1'=8,'lev_0'=8,'lev_1'=2] {'lat_0','lat_1'}, dimensions={1} | all-to-all | bytes 1146880 | tf_op jit(solution)/shard_map/all_to_all | solution.py:21
  39.5 1.8 broadcast_in_dim.45
  41.3 23.2 %all-to-all-start.1 = ((bf16[16,2560,1,2,16]{1,4,3,2,0:T(8,128)(2,1)}), bf16[16,2560,1,2,16]{1,4,3,2,0:T(8,128)(2,1)S(1)}, u32[]{:S(2)}, u32[]{:S(2)}) async-start(bf16[16,2560,1,2,16]{1,4,3,2,0:T(8,128)(2,1)} %broadcast_in_dim.45), calls=%async_computation.1 | async-start | bytes 5242880 | tf_op jit(solution)/shard_map/all_to_all | solution.py:34
  64.5 0.6 dynamic_slice.6
  65.7 58.3 %all-to-all-done.1 = bf16[16,2560,1,2,16]{1,4,3,2,0:T(8,128)(2,1)S(1)} async-done(((bf16[16,2560,1,2,16]{1,4,3,2,0:T(8,128)(2,1)}), bf16[16,2560,1,2,16]{1,4,3,2,0:T(8,128)(2,1)S(1)}, u32[]{:S(2)}, u32[]{:S(2)}) %all-to-all-start.1) | async-done | bytes 2621472 | tf_op jit(solution)/shard_map/all_to_all | solution.py:34
  124.2 0.5 fusion
  124.8 0.6 fusion.3
  125.3 0.7 copy.48
  126.1 5.5 %all-to-all-start.2 = ((f32[1,256,80]{2,0,1:T(1,128)}), f32[1,256,80]{2,0,1:T(1,128)S(1)}, u32[]{:S(2)}, u32[]{:S(2)}) async-start(f32[1,256,80]{2,0,1:T(1,128)} %copy.48), calls=%async_computation.2 | async-start | bytes 262144 | tf_op jit(solution)/shard_map/all_to_all | solution.py:81
  131.6 8.9 %all-to-all-done.2 = f32[1,256,80]{2,0,1:T(1,128)S(1)} async-done(((f32[1,256,80]{2,0,1:T(1,128)}), f32[1,256,80]{2,0,1:T(1,128)S(1)}, u32[]{:S(2)}, u32[]{:S(2)}) %all-to-all-start.2) | async-done | bytes 81952 | tf_op jit(solution)/shard_map/all_to_all | solution.py:81
  140.5 0.7 fusion.4
  141.2 13.4 %psum.28 = f32[]{:T(128)} all-reduce(f32[]{:T(128)} %fusion.4), channel_id=1, replica_groups=mesh['lat_0'=8,'lat_1'=8,'lev_0'=8,'lev_1'=2] {'lat_0'}, use_global_device_ids=true, to_apply=%region_1.3 | all-reduce | flops 1 | bytes 8 | tf_op jit(solution)/shard_map/psum | solution.py:51
  154.6 12.1 %psum.29 = f32[]{:T(128)} all-reduce(f32[]{:T(128)} %psum.28), channel_id=1, replica_groups=mesh['lat_0'=8,'lat_1'=8,'lev_0'=8,'lev_1'=2] {'lat_1'}, use_global_device_ids=true, to_apply=%region_2.4 | all-reduce | flops 1 | bytes 8 | tf_op jit(solution)/shard_map/psum | solution.py:51
  166.7 11.6 %psum.30 = f32[]{:T(128)} all-reduce(f32[]{:T(128)} %psum.29), channel_id=1, replica_groups=mesh['lat_0'=8,'lat_1'=8,'lev_0'=8,'lev_1'=2] {'lev_0'}, use_global_device_ids=true, to_apply=%region_3.5 | all-reduce | flops 1 | bytes 8 | tf_op jit(solution)/shard_map/psum | solution.py:51
  178.4 13.9 %psum.31 = f32[]{:T(128)} all-reduce(f32[]{:T(128)} %psum.30), channel_id=1, replica_groups=mesh['lat_0'=8,'lat_1'=8,'lev_0'=8,'lev_1'=2] {'lev_1'}, use_global_device_ids=true, to_apply=%region_4.6 | all-reduce | flops 1 | bytes 8 | tf_op jit(solution)/shard_map/psum | solution.py:51
  192.3 0.7 all_to_all.37
  (18 shorter events, 2.8 us)
Async XLA Ops:
  41.3 23.2 %copy-start = (s32[64]{0:T(128)S(1)}, s32[64]{0:T(128)}, u32[]{:S(2)}) copy-start(s32[64]{0:T(128)} %param.9) | copy-start | bytes 772
  41.3 82.7 %all-to-all-start.1 = ((bf16[16,2560,1,2,16]{1,4,3,2,0:T(8,128)(2,1)}), bf16[16,2560,1,2,16]{1,4,3,2,0:T(8,128)(2,1)S(1)}, u32[]{:S(2)}, u32[]{:S(2)}) async-start(bf16[16,2560,1,2,16]{1,4,3,2,0:T(8,128)(2,1)} %broadcast_in_dim.45), calls=%async_computation.1 | async-start | bytes 5242880 | tf_op jit(solution)/shard_map/all_to_all | solution.py:34
  126.1 14.4 %all-to-all-start.2 = ((f32[1,256,80]{2,0,1:T(1,128)}), f32[1,256,80]{2,0,1:T(1,128)S(1)}, u32[]{:S(2)}, u32[]{:S(2)}) async-start(f32[1,256,80]{2,0,1:T(1,128)} %copy.48), calls=%async_computation.2 | async-start | bytes 262144 | tf_op jit(solution)/shard_map/all_to_all | solution.py:81
where the time goes:
time: 195 us
  blocking collectives  80.6 us (41%)
  waiting for transfers between devices  67.2 us (34%)
  starting transfers between devices  28.7 us (15%)
  local copies, waits for them, and re-layouts  10.1 us (5%)
  other arithmetic  3.91 us (2%)
  between operations  3.19 us (2%)
    all_to_all x1, waiting for transfers between devices, copy_for_each(): lax.all_to_all(jnp.broadcast_to(value[None], (length, *value.shape)), axi...  58.3 us
    psum x4, blocking collectives, by_axis(): return functools.reduce(lax.psum, axes, value)  51 us
    all_to_all x1, blocking collectives, sent_together(): lax.all_to_all(both, axis, split_axis=split_dim, concat_axis=concat_dim,...  29.6 us
    all_to_all x1, starting transfers between devices, copy_for_each(): lax.all_to_all(jnp.broadcast_to(value[None], (length, *value.shape)), axi...  23.2 us
    all_to_all x1, waiting for transfers between devices, shards(): lax.all_to_all(all_channels, LEV, split_axis=1, concat_axis=2, tiled=True)  8.87 us
    all_to_all x1, starting transfers between devices, shards(): lax.all_to_all(all_channels, LEV, split_axis=1, concat_axis=2, tiled=True)  5.54 us
  transfers between devices with their start and end apart: 2, of which 2 were waited for; matrix products, arithmetic and copies ran while one was open for 0% of the time, Pallas kernels for 0%

commit v1 on v0

v1 whole, which is shorter than its diff:
```python
import functools

import jax
import jax.numpy as jnp
import numpy as np
from jax import lax
from jax.experimental import pallas as pl
from jax.experimental.pallas import tpu as pltpu
from jax.sharding import Mesh
from jax.sharding import PartitionSpec as P

MESH = pl.DeviceIdType.MESH
TRUNC = 1280
M_WIN = 128
SPACING = 10
LAT = ("lat_0", "lat_1")
LEV = ("lev_0", "lev_1")
LANE = 128
SUB = 5
GROUPS = ((0, 3), (3, 5), (5, 7))
TABLE_GROUPS = (0, 1)
WAVE_GROUP = 2


def row_orders(n):
    rows = n * n * SUB
    r = np.arange(rows)
    b, src, l = r // (n * SUB), r // SUB % n, r % SUB
    q1 = np.zeros((rows, rows), np.float32)
    q1[r, src * n * SUB + l * n + b] = 1
    q2 = np.zeros((rows, rows), np.float32)
    q2[r, src * n * SUB + b * SUB + l] = 1
    return q1, q2


def kernel(n, nz, f_hbm, w_smem, leg_hbm, pair_row_hbm, pair_smem, q1_hbm, q2_hbm, out_ref, energy_ref,
           f_in, f_rows, tin, pair_row, q1, q2, z_send, z_recv, p1s, p1r, p2s, p2r, w_sib,
           part, a3, a4, merged, fin, fin_sib, e0, e1, e2,
           load_sem, zs_sem, zr_sem, p1s_sem, p1r_sem, p2s_sem, p2r_sem, w_sem,
           a_ssem, a_rsem, n_ssem, n_rsem, m_ssem, f_sem, e_ssem, e_rsem):
    x, y, z, c = (lax.axis_index(a) for a in LAT + LEV)
    ch = f_in.shape[0]
    half = tin.shape[2]
    chunks = half // LANE
    other = 1 - c
    pairs = n * n

    def core_xy(first, j):
        along_x = (c == 0) if first else (c == 1)
        return (jnp.where(along_x, j, x), jnp.where(along_x, y, j), z, c)

    me_first = jnp.where(c == 0, x, y)
    me_second = jnp.where(c == 0, y, x)

    def wrap(v, size):
        return lax.rem(v + size, size)

    barrier = pltpu.get_barrier_semaphore()
    count = 0
    for r in range(1, n):
        pl.semaphore_signal(barrier, inc=1, device_id=(wrap(x + r, n), y, z, c), device_id_type=MESH)
        pl.semaphore_signal(barrier, inc=1, device_id=(x, wrap(y + r, n), z, c), device_id_type=MESH)
        count += 2
    for r in range(1, nz):
        pl.semaphore_signal(barrier, inc=1, device_id=(x, y, wrap(z + r, nz), c), device_id_type=MESH)
        pl.semaphore_signal(barrier, inc=1, device_id=(x, y, wrap(z + r, nz), other), device_id_type=MESH)
        count += 2
    pl.semaphore_signal(barrier, inc=1, device_id=(x, y, z, other), device_id_type=MESH)
    count += 1

    loads = [
        pltpu.make_async_copy(f_hbm, f_in, load_sem.at[0]),
        pltpu.make_async_copy(
            leg_hbm.at[pl.ds(SUB * z, SUB), :, pl.ds(pl.multiple_of(c * half, LANE), half)], tin, load_sem.at[1]
        ),
        pltpu.make_async_copy(pair_row_hbm, pair_row, load_sem.at[2]),
        pltpu.make_async_copy(q1_hbm, q1, load_sem.at[3]),
        pltpu.make_async_copy(q2_hbm, q2, load_sem.at[4]),
    ]
    for load in loads:
        load.start()

    def remote(src, dst, ssem, rsem, device):
        return pltpu.make_async_remote_copy(
            src_ref=src, dst_ref=dst, send_sem=ssem, recv_sem=rsem, device_id=device, device_id_type=MESH
        )

    loads[0].wait()
    lats = f_in.shape[1]
    f_rows[...] = f_in[...].astype(jnp.float32).reshape(ch * lats, M_WIN)
    for l in range(lats):
        z_send[l // SUB, l % SUB] = f_rows[pl.ds(l, ch, stride=lats), :].astype(jnp.bfloat16)
    z_recv[z] = z_send[z]

    loads[2].wait()
    row_i = lax.broadcasted_iota(jnp.int32, (pairs, pairs), 0)
    col_i = lax.broadcasted_iota(jnp.int32, (pairs, pairs), 1)
    owner_of_col = jnp.where(c == 0, col_i, lax.rem(col_i, n) * n + lax.div(col_i, n))
    order = jnp.where(row_i == owner_of_col, 1.0, 0.0).astype(jnp.bfloat16)
    wave_i = lax.broadcasted_iota(jnp.int32, (M_WIN, pairs), 0)
    ids = jnp.broadcast_to(pair_row[0:1, 0:pairs], (M_WIN, pairs))
    low_hot = jnp.where(wave_i == ids, 1.0, 0.0).astype(jnp.bfloat16)
    high_hot = jnp.where(M_WIN - 1 - wave_i == ids, 1.0, 0.0).astype(jnp.bfloat16)

    def nt(a, b):
        return lax.dot_general(a, b, (((1,), (1,)), ((), ())), preferred_element_type=jnp.float32)

    low_sel = nt(order, low_hot).astype(jnp.bfloat16)
    high_sel = nt(order, high_hot).astype(jnp.bfloat16)

    pl.semaphore_wait(barrier, count)

    far_first = [r for k in range(n // 2, 0, -1) for r in sorted({k, n - k})]
    z_far_first = [r for k in range(nz // 2, 0, -1) for r in sorted({k, nz - k})]
    for r in z_far_first:
        t = wrap(z + r, nz)
        remote(z_send.at[t], z_recv.at[z], zs_sem, zr_sem, (x, y, t, c)).start()

    def send_first(g):
        j0, j1 = GROUPS[g]
        p1r[j0:j1, me_first] = p1s[j0:j1, me_first]
        for r in far_first:
            t = wrap(me_first + r, n)
            remote(
                p1s.at[j0:j1, t], p1r.at[j0:j1, me_first], p1s_sem.at[g], p1r_sem.at[g], core_xy(True, t)
            ).start()

    def forward(g):
        j0, j1 = GROUPS[g]
        if n > 1:
            got = p1r.at[j0:j1, 0 : n - 1]
            remote(got, got, p1s_sem.at[g], p1r_sem.at[g], core_xy(True, me_first)).wait_recv()
        for j in range(j0, j1):
            rows = p1r[j].reshape(n * SUB * n, LANE)
            p2s[j] = jnp.dot(q1[...], rows, preferred_element_type=jnp.float32).astype(jnp.bfloat16).reshape(p2s.shape[1:])
        p2r[j0:j1, me_second] = p2s[j0:j1, me_second]
        for r in far_first:
            t = wrap(me_second + r, n)
            remote(
                p2s.at[j0:j1, t], p2r.at[j0:j1, me_second], p2s_sem.at[g], p2r_sem.at[g], core_xy(False, t)
            ).start()

    def received_second(g):
        j0, j1 = GROUPS[g]
        if n > 1:
            got = p2r.at[j0:j1, 0 : n - 1]
            remote(got, got, p2s_sem.at[g], p2r_sem.at[g], core_xy(False, me_second)).wait_recv()

    loads[1].wait()
    table_sel = low_sel[:, 0:pairs]
    for g in TABLE_GROUPS:
        j0, j1 = GROUPS[g]
        for l in range(SUB):
            rows = jnp.dot(table_sel, tin[l, :, j0 * LANE : j1 * LANE], preferred_element_type=jnp.float32)
            rows = rows.astype(jnp.bfloat16)
            for j in range(j0, j1):
                at = (j - j0) * LANE
                p1s[j, :, l] = rows[:, at : at + LANE].reshape(n, n, LANE)
        send_first(g)

    loads[3].wait()
    loads[4].wait()
    forward(0)

    if nz > 1:
        got = z_recv.at[0 : nz - 1]
        remote(got, got, zs_sem, zr_sem, (x, y, z, c)).wait_recv()
    for l in range(SUB):
        block = z_recv[:, l].reshape(nz * ch, M_WIN)
        weight = w_smem[SUB * z + l]
        p1s[chunks, :, l] = (nt(low_sel, block) * weight).astype(jnp.bfloat16).reshape(n, n, LANE)
        p1s[chunks + 1, :, l] = (nt(high_sel, block) * weight).astype(jnp.bfloat16).reshape(n, n, LANE)
    send_first(WAVE_GROUP)
    forward(1)
    forward(WAVE_GROUP)

    received_second(WAVE_GROUP)
    swap = remote(p2r.at[chunks : chunks + 2], w_sib, w_sem.at[0], w_sem.at[1], (x, y, z, other))
    swap.start()
    for g in TABLE_GROUPS:
        received_second(g)
    rows_of = n * n * SUB
    mine = [p2r[chunks + i].reshape(rows_of, LANE) for i in range(2)]
    swap.wait_recv()
    theirs = [
        jnp.dot(q2[...], w_sib[i].reshape(rows_of, LANE), preferred_element_type=jnp.float32).astype(jnp.bfloat16)
        for i in range(2)
    ]
    waves = jnp.concatenate([mine[0], theirs[0], mine[1], theirs[1]], axis=1)

    limit = TRUNC - SPACING * pair_smem[x * n + y] - SPACING // 2
    for j in range(chunks):
        table = p2r[j].reshape(rows_of, LANE)
        both = lax.dot_general(waves, table, (((0,), (0,)), ((), ())), preferred_element_type=jnp.float32)
        column = c * half + j * LANE + lax.broadcasted_iota(jnp.int32, (2 * LANE, LANE), 1)
        sums = jnp.where(column < limit, both[: 2 * LANE], both[2 * LANE :])
        part[:, :, :, j * LANE : (j + 1) * LANE] = sums.reshape(2, nz, ch, LANE)

    sends = []
    if nz > 1:
        def up(k):
            return wrap(z + k + nz, nz)

        for i, sign in enumerate((1, -1)):
            sends.append(remote(part.at[:, up(3 * sign)], a3.at[i], a_ssem.at[i], a_rsem.at[i], (x, y, up(sign), c)))
            sends.append(remote(part.at[i, up(4)], a4.at[i], a_ssem.at[2 + i], a_rsem.at[2 + i], (x, y, up(2 * sign), c)))
        for i, sign in enumerate((1, -1)):
            for h in range(2):
                to = (x, y, up(sign), jnp.where(h == 0, c, other))
                sends.append(remote(part.at[h, up(sign)], fin.at[h, i], n_ssem.at[h, i], n_rsem.at[h, i], to))
    own = remote(part.at[1, z], fin_sib, f_sem.at[0], f_sem.at[1], (x, y, z, other))
    for send in sends:
        send.start()
    own.start()
    if nz > 1:
        late = []
        for i, sign in enumerate((1, -1)):
            remote(a3.at[i], a3.at[i], a_ssem.at[i], a_rsem.at[i], (x, y, z, c)).wait_recv()
            remote(a4.at[i], a4.at[i], a_ssem.at[2 + i], a_rsem.at[2 + i], (x, y, z, c)).wait_recv()
            merged[i] = part[:, up(2 * sign)] + a3[i]
            merged[i, i] = merged[i, i] + a4[i]
            for h in range(2):
                to = (x, y, up(2 * sign), jnp.where(h == 0, c, other))
                send = remote(merged.at[i, h], fin.at[h, 2 + i], m_ssem.at[h, i], n_rsem.at[h, 2 + i], to)
                send.start()
                late.append(send)
        sends = sends + late
    own.wait_recv()
    total = [part[0, z], fin_sib[...]]
    if nz > 1:
        for i in range(4):
            for h in range(2):
                remote(fin.at[h, i], fin.at[h, i], f_sem.at[0], n_rsem.at[h, i], (x, y, z, c)).wait_recv()
                total[h] = total[h] + fin[h, i]

    out_ref[:, pl.ds(pl.multiple_of(c * half, LANE), half)] = total[0]
    out_ref[:, pl.ds(pl.multiple_of(other * half, LANE), half)] = total[1]
    levels = nz * 2 * ch // 2
    channel = (z * 2 + c) * ch + lax.broadcasted_iota(jnp.int32, (ch, half), 0)
    factor = 1.0 + 2.0 * lax.shift_right_logical(channel, 1).astype(jnp.float32) / (levels - 1)
    squares = factor * (total[0] * total[0] + total[1] * total[1])
    tile = jnp.zeros((8, LANE), jnp.float32)
    for i in range(ch // 8):
        for j in range(chunks):
            tile = tile + squares[i * 8 : i * 8 + 8, j * LANE : (j + 1) * LANE]

    def added(ref, size, at, tile, sem, devices):
        ref[at] = tile
        for device in devices:
            remote(ref.at[at], ref.at[at], e_ssem.at[sem], e_rsem.at[sem], device).start()
        if size > 1:
            got = ref.at[0 : size - 1]
            remote(got, got, e_ssem.at[sem], e_rsem.at[sem], (x, y, z, c)).wait_recv()
        tile = ref[0]
        for i in range(1, size):
            tile = tile + ref[i]
        return tile

    peers = [(x, y, wrap(z + r, nz), k) for r in z_far_first for k in (c, other)] + [(x, y, z, other)]
    tile = added(e0, nz * 2, z * 2 + c, tile, 0, peers)
    tile = added(e1, n, y, tile, 1, [(x, wrap(y + r, n), z, c) for r in far_first])
    tile = added(e2, n, x, tile, 2, [(wrap(x + r, n), y, z, c) for r in far_first])
    energy_ref[0, 0] = jnp.sum(tile) / (pairs * 2 * levels * 2 * half)

    if nz > 1:
        gone = z_send.at[0 : nz - 1]
        remote(gone, gone, zs_sem, zr_sem, (x, y, z, c)).wait_send()
    if n > 1:
        for g, (j0, j1) in enumerate(GROUPS):
            gone = p1s.at[j0:j1, 0 : n - 1]
            remote(gone, gone, p1s_sem.at[g], p1r_sem.at[g], (x, y, z, c)).wait_send()
            gone = p2s.at[j0:j1, 0 : n - 1]
            remote(gone, gone, p2s_sem.at[g], p2r_sem.at[g], (x, y, z, c)).wait_send()
    swap.wait_send()
    own.wait_send()
    for send in sends:
        send.wait_send()
    for sem, ref, size in ((0, e0, nz * 2), (1, e1, n), (2, e2, n)):
        if size > 1:
            gone = ref.at[0 : size - 1]
            remote(gone, gone, e_ssem.at[sem], e_rsem.at[sem], (x, y, z, c)).wait_send()


def shards(n, nz, fourier, quad_weights, legendre, owner_pair):
    ch, lats, _ = fourier.shape
    _, pairs, length = legendre.shape
    half = length // 2
    chunks = half // LANE
    rows = n * n * SUB
    q1, q2 = row_orders(n)
    pair_row = jnp.pad(owner_pair, (0, LANE - pairs)).reshape(1, LANE)
    bf16, f32 = jnp.bfloat16, jnp.float32
    vmem, dma = pltpu.VMEM, pltpu.SemaphoreType.DMA
    any_space = pl.BlockSpec(memory_space=pl.ANY)
    smem = pl.BlockSpec(memory_space=pltpu.SMEM)
    exchange = (chunks + 2, n, SUB, n, LANE)
    spectra, energy = pl.pallas_call(
        functools.partial(kernel, n, nz),
        out_shape=(
            jax.ShapeDtypeStruct((ch, length), f32),
            jax.ShapeDtypeStruct((1, 1), f32),
        ),
        in_specs=[any_space, smem, any_space, any_space, smem, any_space, any_space],
        out_specs=(pl.BlockSpec(memory_space=pltpu.VMEM), smem),
        scratch_shapes=[
            vmem((ch, lats, M_WIN), bf16),
            vmem((ch * lats, M_WIN), f32),
            vmem((SUB, pairs, half), bf16),
            vmem((1, LANE), jnp.int32),
            vmem((rows, rows), bf16),
            vmem((rows, rows), bf16),
            vmem((nz, SUB, ch, M_WIN), bf16),
            vmem((nz, SUB, ch, M_WIN), bf16),
            vmem(exchange, bf16),
            vmem(exchange, bf16),
            vmem(exchange, bf16),
            vmem(exchange, bf16),
            vmem((2, *exchange[1:]), bf16),
            vmem((2, nz, ch, half), f32),
            vmem((2, 2, ch, half), f32),
            vmem((2, ch, half), f32),
            vmem((2, 2, ch, half), f32),
            vmem((2, 4, ch, half), f32),
            vmem((ch, half), f32),
            vmem((nz * 2, 8, LANE), f32),
            vmem((n, 8, LANE), f32),
            vmem((n, 8, LANE), f32),
            dma((5,)),
            dma,
            dma,
            dma((3,)),
            dma((3,)),
            dma((3,)),
            dma((3,)),
            dma((2,)),
            dma((4,)),
            dma((4,)),
            dma((2, 2)),
            dma((2, 4)),
            dma((2, 2)),
            dma((2,)),
            dma((3,)),
            dma((3,)),
        ],
        compiler_params=pltpu.CompilerParams(
            collective_id=0, has_side_effects=True, vmem_limit_bytes=40 * 1024 * 1024
        ),
        name="legendre",
    )(fourier, quad_weights, legendre, pair_row, owner_pair, jnp.asarray(q1, bf16), jnp.asarray(q2, bf16))
    return spectra[None], energy[0, 0]


def solution(mesh):
    n = round(mesh.shape["lat"] ** 0.5)
    nz = mesh.shape["lev"] // 2
    finer = Mesh(mesh.devices.reshape(n, n, nz, 2), LAT + LEV)
    return jax.shard_map(
        functools.partial(shards, n, nz),
        mesh=finer,
        in_specs=(P(LEV, LAT, None), P(LAT), P(LAT, None, None), P()),
        out_specs=(P(LAT, LEV, None), P()),
        check_vma=False,
    )
```

time: 195 us -> 80.8 us (0.41)
  blocking collectives: 80.6 us -> 0 us
  Pallas kernels: 0 us -> 69.5 us
  waiting for transfers between devices: 67.2 us -> 0 us
  starting transfers between devices: 28.7 us -> 0 us
  other arithmetic: 3.91 us -> 0 us
    pallas_call x0 -> x1, Pallas kernels: none -> 69.5 us  [shards(): pl.pallas_call(functools.partial(kernel, n, nz), out_shape=(jax.ShapeDtyp...]
    all_to_all x2 -> x0, waiting for transfers between devices: 67.2 us -> none  [the longest x1 58.3 us: copy_for_each(): lax.all_to_all(jnp.broadcast_to(value[None], (length, *value.shape)), axi...]
    psum x4 -> x0, blocking collectives: 51 us -> none  [by_axis(): return functools.reduce(lax.psum, axes, value)]
    all_to_all x1 -> x0, blocking collectives: 29.6 us -> none  [sent_together(): lax.all_to_all(both, axis, split_axis=split_dim, concat_axis=concat_dim,...]
    all_to_all x2 -> x0, starting transfers between devices: 28.7 us -> none  [the longest x1 23.2 us: copy_for_each(): lax.all_to_all(jnp.broadcast_to(value[None], (length, *value.shape)), axi...]
    unnamed x3 -> x13, local copies, waits for them, and re-layouts: 0.43 us -> 7.61 us
    dynamic_slice x2 -> x0, local copies, waits for them, and re-layouts: 2.19 us -> none  [the longest x1 1.6 us: shards(): lax.dynamic_slice_in_dim(legendre, first_column, slice_len, 2)]
    gather x3 -> x0, local copies, waits for them, and re-layouts: 1.96 us -> none  [the longest x1 0.69 us: shards(): legendre_part = jnp.take(column_block, owner_pair, axis=1)]
  transfers between devices with their start and end apart: 2 -> 0, of which waited for: 2 -> 0; matrix products, arithmetic and copies ran while one was open for 0% -> 0% of each run, Pallas kernels for 0% -> 0%
where the time goes in v1:
time: 80.8 us; the launch traced here: 80.3 us
  Pallas kernels  69.5 us (86%)
  local copies, waits for them, and re-layouts  8.27 us (10%)
  between operations  2.46 us (3%)
    pallas_call x1, Pallas kernels, shards(): pl.pallas_call(functools.partial(kernel, n, nz), out_shape=(jax.ShapeDtyp...  69.5 us
    unnamed x13, local copies, waits for them, and re-layouts  7.61 us

profile of v1, /device:TPU:1, one launch (start us, length us, event | category | flops | bytes accessed | tf_op | source)
XLA Modules:
  0.0 80.3 jit_solution(9137582277736530118)
XLA Ops:
  0.6 0.7 pad_bitcast_fusion.pair_row_hbm
  1.3 0.0 copy-start
  1.3 2.9 %copy-done = bf16[40,64,1280]{2,1,0:T(8,128)(2,1)S(1)} copy-done((bf16[40,64,1280]{2,1,0:T(8,128)(2,1)S(1)}, bf16[40,64,1280]{2,1,0:T(8,128)(2,1)}, u32[]{:S(2)}) %copy-start) | copy-done | bytes 6553624
  4.1 0.0 copy-start.1
  4.2 0.9 %copy-done.1 = bf16[320,320]{1,0:T(8,128)(2,1)S(1)} copy-done((bf16[320,320]{1,0:T(8,128)(2,1)S(1)}, bf16[320,320]{1,0:T(8,128)(2,1)}, u32[]{:S(2)}) %copy-start.1) | copy-done | bytes 204824
  5.1 0.0 copy-start.2
  5.1 0.9 %copy-done.2 = bf16[320,320]{1,0:T(8,128)(2,1)S(1)} copy-done((bf16[320,320]{1,0:T(8,128)(2,1)S(1)}, bf16[320,320]{1,0:T(8,128)(2,1)}, u32[]{:S(2)}) %copy-start.2) | copy-done | bytes 204824
  6.0 0.0 copy-start.3
  6.0 0.9 %copy-done.3 = bf16[16,40,128]{2,1,0:T(8,128)(2,1)S(1)} copy-done((bf16[16,40,128]{2,1,0:T(8,128)(2,1)S(1)}, bf16[16,40,128]{2,1,0:T(8,128)(2,1)}, u32[]{:S(2)}) %copy-start.3) | copy-done | bytes 163864
  7.0 0.0 copy-start.4
  7.0 0.7 copy-done.4
  7.6 0.0 copy-start.5
  7.6 0.7 copy-done.5
  8.3 69.5 %legendre.1 = (f32[16,1280]{1,0:T(8,128)S(1)}, f32[1,1]{1,0:T(1,128)}) custom-call(bf16[16,40,128]{2,1,0:T(8,128)(2,1)S(1)} %copy-done.3, f32[40]{0:T(128)S(1)} %copy-done.4, bf16[40,64,1280]{2,1,0:T(8,128)(2,1)S(1)} %copy-done, s32[1,128]{1,0:T(1,128)S(1)} %pad_bitcast_fusion.pair_row_hbm, s32[64]{0:T(128)S(1)} %copy-done.5, ...), custom_call_target="tpu_custom_call" | custom-call | tf_op jit(solution)/shard_map/legendre/pallas_call | solution.py:297
  77.8 0.6 copy.10
Async XLA Ops:
  1.3 2.9 %copy-start = (bf16[40,64,1280]{2,1,0:T(8,128)(2,1)S(1)}, bf16[40,64,1280]{2,1,0:T(8,128)(2,1)}, u32[]{:S(2)}) copy-start(bf16[40,64,1280]{2,1,0:T(8,128)(2,1)} %leg_hbm.1) | copy-start | bytes 19660804
  4.1 0.9 %copy-start.1 = (bf16[320,320]{1,0:T(8,128)(2,1)S(1)}, bf16[320,320]{1,0:T(8,128)(2,1)}, u32[]{:S(2)}) copy-start(bf16[320,320]{1,0:T(8,128)(2,1)} %constant.7.clone.q2_hbm) | copy-start | bytes 614404
  5.1 0.9 %copy-start.2 = (bf16[320,320]{1,0:T(8,128)(2,1)S(1)}, bf16[320,320]{1,0:T(8,128)(2,1)}, u32[]{:S(2)}) copy-start(bf16[320,320]{1,0:T(8,128)(2,1)} %constant.6.clone.q1_hbm) | copy-start | bytes 614404
  6.0 0.9 %copy-start.3 = (bf16[16,40,128]{2,1,0:T(8,128)(2,1)S(1)}, bf16[16,40,128]{2,1,0:T(8,128)(2,1)}, u32[]{:S(2)}) copy-start(bf16[16,40,128]{2,1,0:T(8,128)(2,1)} %f_hbm.1) | copy-start | bytes 491524
  7.0 0.7 copy-start.4
  7.6 0.7 copy-start.5

commit v2 on v1

v2 whole, which is shorter than its diff:
```python
import functools

import jax
import jax.numpy as jnp
import numpy as np
from jax import lax
from jax.experimental import pallas as pl
from jax.experimental.pallas import tpu as pltpu
from jax.sharding import Mesh
from jax.sharding import PartitionSpec as P

MESH = pl.DeviceIdType.MESH
TRUNC = 1280
M_WIN = 128
SPACING = 10
LAT = ("lat_0", "lat_1")
LEV = ("lev_0", "lev_1")
LANE = 128
SUB = 5
GROUPS = ((0, 1), (1, 3), (3, 5), (5, 7))
TABLE_GROUPS = (0, 1, 2)
WAVE_GROUP = 3
EARLY = (0,)
LATE = (1, 2)


def row_orders(n):
    rows = n * n * SUB
    r = np.arange(rows)
    b, src, l = r // (n * SUB), r // SUB % n, r % SUB
    q1 = np.zeros((rows, rows), np.float32)
    q1[r, src * n * SUB + l * n + b] = 1
    q2 = np.zeros((rows, rows), np.float32)
    q2[r, src * n * SUB + b * SUB + l] = 1
    return q1, q2


def kernel(n, nz, f_hbm, w_hbm, leg_hbm, pair_row_hbm, pair_hbm, q1_hbm, q2_hbm, out_hbm, energy_ref,
           f_in, f_rows, tin, pair_row, pair_smem, w_smem, q1, q2, z_send, z_recv, p1s, p1r, p2s, p2r, t_sib,
           t_perm, part, a3, a4, merged, fin, out_buf, e0, e1, e2,
           load_sem, zs_sem, zr_sem, p1s_sem, p1r_sem, p2s_sem, p2r_sem, t_ssem, t_rsem,
           a_ssem, a_rsem, f_ssem, f_rsem, e_ssem, e_rsem):
    x, y, z, c = (lax.axis_index(a) for a in LAT + LEV)
    ch = f_in.shape[0]
    half = tin.shape[2]
    chunks = half // LANE
    other = 1 - c
    pairs = n * n
    rows_of = n * n * SUB

    def core_xy(first, j):
        along_x = (c == 0) if first else (c == 1)
        return (jnp.where(along_x, j, x), jnp.where(along_x, y, j), z, c)

    me_first = jnp.where(c == 0, x, y)
    me_second = jnp.where(c == 0, y, x)

    def wrap(v, size):
        return lax.rem(v + size, size)

    loads = [
        pltpu.make_async_copy(f_hbm, f_in, load_sem.at[0]),
        pltpu.make_async_copy(pair_row_hbm, pair_row, load_sem.at[2]),
        pltpu.make_async_copy(
            leg_hbm.at[pl.ds(SUB * z, SUB), :, pl.ds(pl.multiple_of(c * half, LANE), half)], tin, load_sem.at[1]
        ),
        pltpu.make_async_copy(q1_hbm, q1, load_sem.at[3]),
        pltpu.make_async_copy(w_hbm, w_smem, load_sem.at[5]),
        pltpu.make_async_copy(pair_hbm, pair_smem, load_sem.at[6]),
        pltpu.make_async_copy(q2_hbm, q2, load_sem.at[4]),
    ]
    for load in loads:
        load.start()
    f_load, pair_row_load, table_load, q1_load, w_load, pair_load, q2_load = loads

    barrier = pltpu.get_barrier_semaphore()
    count = 0
    for r in range(1, n):
        pl.semaphore_signal(barrier, inc=1, device_id=(wrap(x + r, n), y, z, c), device_id_type=MESH)
        pl.semaphore_signal(barrier, inc=1, device_id=(x, wrap(y + r, n), z, c), device_id_type=MESH)
        count += 2
    for r in range(1, nz):
        pl.semaphore_signal(barrier, inc=1, device_id=(x, y, wrap(z + r, nz), c), device_id_type=MESH)
        pl.semaphore_signal(barrier, inc=1, device_id=(x, y, wrap(z + r, nz), other), device_id_type=MESH)
        count += 2
    pl.semaphore_signal(barrier, inc=1, device_id=(x, y, z, other), device_id_type=MESH)
    count += 1

    def remote(src, dst, ssem, rsem, device):
        return pltpu.make_async_remote_copy(
            src_ref=src, dst_ref=dst, send_sem=ssem, recv_sem=rsem, device_id=device, device_id_type=MESH
        )

    f_load.wait()
    lats = f_in.shape[1]
    f_rows[...] = f_in[...].astype(jnp.float32).reshape(ch * lats, M_WIN)
    for l in range(lats):
        z_send[l // SUB, l % SUB] = f_rows[pl.ds(l, ch, stride=lats), :].astype(jnp.bfloat16)
    z_recv[z] = z_send[z]

    pl.semaphore_wait(barrier, count)

    far_first = [r for k in range(n // 2, 0, -1) for r in sorted({k, n - k})]
    z_far_first = [r for k in range(nz // 2, 0, -1) for r in sorted({k, nz - k})]
    for r in z_far_first:
        t = wrap(z + r, nz)
        remote(z_send.at[t], z_recv.at[z], zs_sem, zr_sem, (x, y, t, c)).start()

    pair_row_load.wait()
    row_i = lax.broadcasted_iota(jnp.int32, (pairs, pairs), 0)
    col_i = lax.broadcasted_iota(jnp.int32, (pairs, pairs), 1)
    owner_of_col = jnp.where(c == 0, col_i, lax.rem(col_i, n) * n + lax.div(col_i, n))
    order = jnp.where(row_i == owner_of_col, 1.0, 0.0).astype(jnp.bfloat16)
    wave_i = lax.broadcasted_iota(jnp.int32, (M_WIN, pairs), 0)
    ids = jnp.broadcast_to(pair_row[...], (M_WIN, pairs))
    low_hot = jnp.where(wave_i == ids, 1.0, 0.0).astype(jnp.bfloat16)
    high_hot = jnp.where(M_WIN - 1 - wave_i == ids, 1.0, 0.0).astype(jnp.bfloat16)

    def nt(a, b):
        return lax.dot_general(a, b, (((1,), (1,)), ((), ())), preferred_element_type=jnp.float32)

    low_sel = nt(order, low_hot).astype(jnp.bfloat16)
    high_sel = nt(order, high_hot).astype(jnp.bfloat16)

    def send_first(g):
        j0, j1 = GROUPS[g]
        p1r[j0:j1, me_first] = p1s[j0:j1, me_first]
        for r in far_first:
            t = wrap(me_first + r, n)
            remote(
                p1s.at[j0:j1, t], p1r.at[j0:j1, me_first], p1s_sem.at[g], p1r_sem.at[g], core_xy(True, t)
            ).start()

    def forward(g):
        j0, j1 = GROUPS[g]
        if n > 1:
            got = p1r.at[j0:j1, 0 : n - 1]
            remote(got, got, p1s_sem.at[g], p1r_sem.at[g], core_xy(True, me_first)).wait_recv()
        for j in range(j0, j1):
            rows = p1r[j].reshape(rows_of, LANE)
            p2s[j] = jnp.dot(q1[...], rows, preferred_element_type=jnp.float32).astype(jnp.bfloat16).reshape(p2s.shape[1:])
        p2r[j0:j1, me_second] = p2s[j0:j1, me_second]
        for r in far_first:
            t = wrap(me_second + r, n)
            remote(
                p2s.at[j0:j1, t], p2r.at[j0:j1, me_second], p2s_sem.at[g], p2r_sem.at[g], core_xy(False, t)
            ).start()

    def received_second(g):
        j0, j1 = GROUPS[g]
        if n > 1:
            got = p2r.at[j0:j1, 0 : n - 1]
            remote(got, got, p2s_sem.at[g], p2r_sem.at[g], core_xy(False, me_second)).wait_recv()

    table_load.wait()
    table_sel = low_sel[:, 0:pairs]
    for g in TABLE_GROUPS:
        j0, j1 = GROUPS[g]
        for l in range(SUB):
            rows = jnp.dot(table_sel, tin[l, :, j0 * LANE : j1 * LANE], preferred_element_type=jnp.float32)
            rows = rows.astype(jnp.bfloat16)
            for j in range(j0, j1):
                at = (j - j0) * LANE
                p1s[j, :, l] = rows[:, at : at + LANE].reshape(n, n, LANE)
        send_first(g)

    for load in (q1_load, w_load, pair_load, q2_load):
        load.wait()
    for g in EARLY:
        forward(g)

    if nz > 1:
        got = z_recv.at[0 : nz - 1]
        remote(got, got, zs_sem, zr_sem, (x, y, z, c)).wait_recv()
    for l in range(SUB):
        block = z_recv[:, l].reshape(nz * ch, M_WIN)
        weight = w_smem[SUB * z + l]
        p1s[chunks, :, l] = (nt(low_sel, block) * weight).astype(jnp.bfloat16).reshape(n, n, LANE)
        p1s[chunks + 1, :, l] = (nt(high_sel, block) * weight).astype(jnp.bfloat16).reshape(n, n, LANE)
    send_first(WAVE_GROUP)
    for g in LATE:
        forward(g)
    forward(WAVE_GROUP)

    swaps = []
    for g in TABLE_GROUPS:
        received_second(g)
        j0, j1 = GROUPS[g]
        swap = remote(p2r.at[j0:j1], t_sib.at[j0:j1], t_ssem.at[g], t_rsem.at[g], (x, y, z, other))
        swap.start()
        swaps.append(swap)
    for g in TABLE_GROUPS:
        swaps[g].wait_recv()
        for j in range(*GROUPS[g]):
            rows = t_sib[j].reshape(rows_of, LANE)
            t_perm[j] = jnp.dot(q2[...], rows, preferred_element_type=jnp.float32).astype(jnp.bfloat16)

    received_second(WAVE_GROUP)
    waves = jnp.concatenate([p2r[chunks + i].reshape(rows_of, LANE) for i in range(2)], axis=1)
    limit = TRUNC - SPACING * pair_smem[x * n + y] - SPACING // 2
    for j in range(0, 2 * chunks, 2):
        blocks = [p2r[i].reshape(rows_of, LANE) if i < chunks else t_perm[i - chunks] for i in (j, j + 1)]
        table = jnp.concatenate(blocks, axis=1)
        both = lax.dot_general(waves, table, (((0,), (0,)), ((), ())), preferred_element_type=jnp.float32)
        for i in range(2):
            first = c * half + (j + i) * LANE if j + i < chunks else other * half + (j + i - chunks) * LANE
            column = first + lax.broadcasted_iota(jnp.int32, (LANE, LANE), 1)
            at = i * LANE
            sums = jnp.where(column < limit, both[:LANE, at : at + LANE], both[LANE:, at : at + LANE])
            part[:, :, (j + i) * LANE : (j + i + 1) * LANE] = sums.reshape(nz, ch, LANE)

    def up(k):
        return wrap(z + k + nz, nz)

    ways = ((0, 1), (1, -1)) if nz > 1 else ()
    sends = []
    for i, sign in ways:
        sends.append(remote(part.at[up(3 * sign)], a3.at[i], a_ssem.at[i], a_rsem.at[i], (x, y, up(sign), c)))
        sends.append(remote(
            part.at[up(4), :, i * half : (i + 1) * half], a4.at[i], a_ssem.at[2 + i], a_rsem.at[2 + i],
            (x, y, up(2 * sign), c),
        ))
    for i, sign in ways:
        sends.append(remote(part.at[up(sign)], fin.at[i], f_ssem.at[i], f_rsem.at[i], (x, y, up(sign), c)))
    for send in sends:
        send.start()
    for i, sign in ways:
        sends[2 * i].wait_recv()
        merged[i] = part[up(2 * sign)] + a3[i]
        sends[2 * i + 1].wait_recv()
        merged[i, :, i * half : (i + 1) * half] = merged[i, :, i * half : (i + 1) * half] + a4[i]
        send = remote(merged.at[i], fin.at[2 + i], f_ssem.at[2 + i], f_rsem.at[2 + i], (x, y, up(2 * sign), c))
        send.start()
        sends.append(send)
    total = part[z]
    for send in sends[4:]:
        send.wait_recv()
    for i in range(4 if nz > 1 else 0):
        total = total + fin[i]

    levels = nz * 2 * ch // 2
    channel = (z * 2 + c) * ch + lax.broadcasted_iota(jnp.int32, (ch, LANE), 0)
    factor = 1.0 + 2.0 * lax.shift_right_logical(channel, 1).astype(jnp.float32) / (levels - 1)
    columns = [total[:, j * LANE : (j + 1) * LANE] for j in range(2 * chunks)]
    squares = columns[0] * columns[0]
    for column in columns[1:]:
        squares = squares + column * column
    squares = factor * squares
    tile = squares[0:8]
    for i in range(1, ch // 8):
        tile = tile + squares[i * 8 : i * 8 + 8]

    def share(ref, at, tile, sem, devices):
        ref[at] = tile
        for device in devices:
            remote(ref.at[at], ref.at[at], e_ssem.at[sem], e_rsem.at[sem], device).start()

    def added(ref, size, sem):
        if size > 1:
            got = ref.at[0 : size - 1]
            remote(got, got, e_ssem.at[sem], e_rsem.at[sem], (x, y, z, c)).wait_recv()
        tile = ref[0]
        for i in range(1, size):
            tile = tile + ref[i]
        return tile

    peers = [(x, y, wrap(z + r, nz), k) for r in z_far_first for k in (c, other)] + [(x, y, z, other)]
    share(e0, z * 2 + c, tile, 0, peers)
    out_buf[:, pl.ds(pl.multiple_of(c * half, LANE), half)] = total[:, :half]
    out_buf[:, pl.ds(pl.multiple_of(other * half, LANE), half)] = total[:, half:]
    out_copy = pltpu.make_async_copy(out_buf, out_hbm, load_sem.at[7])
    out_copy.start()
    tile = added(e0, nz * 2, 0)
    share(e1, y, tile, 1, [(x, wrap(y + r, n), z, c) for r in far_first])
    tile = added(e1, n, 1)
    share(e2, x, tile, 2, [(wrap(x + r, n), y, z, c) for r in far_first])
    tile = added(e2, n, 2)
    energy_ref[0, 0] = jnp.sum(tile) / (pairs * 2 * levels * 2 * half)

    out_copy.wait()
    if nz > 1:
        gone = z_send.at[0 : nz - 1]
        remote(gone, gone, zs_sem, zr_sem, (x, y, z, c)).wait_send()
    if n > 1:
        for g, (j0, j1) in enumerate(GROUPS):
            gone = p1s.at[j0:j1, 0 : n - 1]
            remote(gone, gone, p1s_sem.at[g], p1r_sem.at[g], (x, y, z, c)).wait_send()
            gone = p2s.at[j0:j1, 0 : n - 1]
            remote(gone, gone, p2s_sem.at[g], p2r_sem.at[g], (x, y, z, c)).wait_send()
    for send in swaps + sends:
        send.wait_send()
    for sem, ref, size in ((0, e0, nz * 2), (1, e1, n), (2, e2, n)):
        if size > 1:
            gone = ref.at[0 : size - 1]
            remote(gone, gone, e_ssem.at[sem], e_rsem.at[sem], (x, y, z, c)).wait_send()


def shards(n, nz, fourier, quad_weights, legendre, owner_pair):
    ch, lats, _ = fourier.shape
    _, pairs, length = legendre.shape
    half = length // 2
    chunks = half // LANE
    rows = n * n * SUB
    groups = len(GROUPS)
    q1, q2 = row_orders(n)
    bf16, f32 = jnp.bfloat16, jnp.float32
    vmem, dma = pltpu.VMEM, pltpu.SemaphoreType.DMA
    hbm = pl.BlockSpec(memory_space=pltpu.HBM)
    smem = pl.BlockSpec(memory_space=pltpu.SMEM)
    exchange = (chunks + 2, n, SUB, n, LANE)
    spectra, energy = pl.pallas_call(
        functools.partial(kernel, n, nz),
        out_shape=(
            jax.ShapeDtypeStruct((ch, length), f32),
            jax.ShapeDtypeStruct((1, 1), f32),
        ),
        in_specs=[hbm] * 7,
        out_specs=(hbm, smem),
        scratch_shapes=[
            vmem((ch, lats, M_WIN), bf16),
            vmem((ch * lats, M_WIN), f32),
            vmem((SUB, pairs, half), bf16),
            vmem((1, pairs), jnp.int32),
            pltpu.SMEM((pairs,), jnp.int32),
            pltpu.SMEM((lats,), f32),
            vmem((rows, rows), bf16),
            vmem((rows, rows), bf16),
            vmem((nz, SUB, ch, M_WIN), bf16),
            vmem((nz, SUB, ch, M_WIN), bf16),
            vmem(exchange, bf16),
            vmem(exchange, bf16),
            vmem(exchange, bf16),
            vmem(exchange, bf16),
            vmem((chunks, *exchange[1:]), bf16),
            vmem((chunks, rows, LANE), bf16),
            vmem((nz, ch, length), f32),
            vmem((2, ch, length), f32),
            vmem((2, ch, half), f32),
            vmem((2, ch, length), f32),
            vmem((4, ch, length), f32),
            vmem((ch, length), f32),
            vmem((nz * 2, 8, LANE), f32),
            vmem((n, 8, LANE), f32),
            vmem((n, 8, LANE), f32),
            dma((8,)),
            dma,
            dma,
            dma((groups,)),
            dma((groups,)),
            dma((groups,)),
            dma((groups,)),
            dma((groups,)),
            dma((groups,)),
            dma((4,)),
            dma((4,)),
            dma((4,)),
            dma((4,)),
            dma((3,)),
            dma((3,)),
        ],
        compiler_params=pltpu.CompilerParams(
            collective_id=0, has_side_effects=True, vmem_limit_bytes=67_043_328
        ),
        name="legendre",
    )(fourier, quad_weights, legendre, owner_pair.reshape(1, pairs), owner_pair, jnp.asarray(q1, bf16), jnp.asarray(q2, bf16))
    return spectra[None], energy[0, 0]


def solution(mesh):
    n = round(mesh.shape["lat"] ** 0.5)
    nz = mesh.shape["lev"] // 2
    finer = Mesh(mesh.devices.reshape(n, n, nz, 2), LAT + LEV)
    return jax.shard_map(
        functools.partial(shards, n, nz),
        mesh=finer,
        in_specs=(P(LEV, LAT, None), P(LAT), P(LAT, None, None), P()),
        out_specs=(P(LAT, LEV, None), P()),
        check_vma=False,
    )
```

time: 80.8 us -> 72.1 us (0.89)
  local copies, waits for them, and re-layouts: 8.27 us -> 1.53 us
  Pallas kernels: 69.5 us -> 67.7 us
    unnamed x13 -> x1, local copies, waits for them, and re-layouts: 7.61 us -> 1.53 us
    pallas_call x1, Pallas kernels: 69.5 us -> 67.7 us  [shards(): pl.pallas_call(functools.partial(kernel, n, nz), out_shape=(jax.ShapeDtyp...]
where the time goes in v2:
time: 72.1 us; the launch traced here: 71.5 us
  Pallas kernels  67.7 us (94%)
  between operations  2.33 us (3%)
  local copies, waits for them, and re-layouts  1.53 us (2%)
    pallas_call x1, Pallas kernels, shards(): pl.pallas_call(functools.partial(kernel, n, nz), out_shape=(jax.ShapeDtyp...  67.7 us
    unnamed x1, local copies, waits for them, and re-layouts  1.53 us

profile of v2, /device:TPU:1, one launch (start us, length us, event | category | flops | bytes accessed | tf_op | source)
XLA Modules:
  0.0 71.5 jit_solution(12017891216665295290)
XLA Ops:
  0.6 67.7 %legendre.1 = (f32[16,1280]{1,0:T(8,128)}, f32[1,1]{1,0:T(1,128)}) custom-call(bf16[16,40,128]{2,1,0:T(8,128)(2,1)} %f_hbm.1, f32[40]{0:T(128)} %w_hbm.1, bf16[40,64,1280]{2,1,0:T(8,128)(2,1)} %leg_hbm.1, s32[1,64]{1,0:T(1,128)} %bitcast.4, s32[64]{0:T(128)} %pair_hbm.1, bf16[320,320]{1,0:T(8,128)(2,1)} %constant.4.clone.q1_hbm, ...), custom_call_target="tpu_custom_call" | custom-call | tf_op jit(solution)/shard_map/legendre/pallas_call | solution.py:311
  68.3 1.5 %copy.10 = f32[1,16,1280]{2,1,0:T(8,128)} copy(f32[1,16,1280]{2,1,0:T(8,128)} %bitcast.3) | data formatting | bytes 163840

commit v3 on v2

--- a/solution.py
+++ b/solution.py
@@ -17,11 +17,9 @@
 LEV = ("lev_0", "lev_1")
 LANE = 128
 SUB = 5
-GROUPS = ((0, 1), (1, 3), (3, 5), (5, 7))
+GROUPS = ((0, 1), (1, 3), (3, 5), (5, 6), (6, 7))
 TABLE_GROUPS = (0, 1, 2)
-WAVE_GROUP = 3
-EARLY = (0,)
-LATE = (1, 2)
+WAVE_GROUPS = (3, 4)
 
 
 def row_orders(n):
@@ -37,11 +35,12 @@
 
 def kernel(n, nz, f_hbm, w_hbm, leg_hbm, pair_row_hbm, pair_hbm, q1_hbm, q2_hbm, out_hbm, energy_ref,
            f_in, f_rows, tin, pair_row, pair_smem, w_smem, q1, q2, z_send, z_recv, p1s, p1r, p2s, p2r, t_sib,
-           t_perm, part, a3, a4, merged, fin, out_buf, e0, e1, e2,
+           t_perm, part, a3, a4, merged, fin, out_buf, e0, e1,
            load_sem, zs_sem, zr_sem, p1s_sem, p1r_sem, p2s_sem, p2r_sem, t_ssem, t_rsem,
            a_ssem, a_rsem, f_ssem, f_rsem, e_ssem, e_rsem):
     x, y, z, c = (lax.axis_index(a) for a in LAT + LEV)
     ch = f_in.shape[0]
+    part_ch = ch // 2
     half = tin.shape[2]
     chunks = half // LANE
     other = 1 - c
@@ -95,16 +94,19 @@
     lats = f_in.shape[1]
     f_rows[...] = f_in[...].astype(jnp.float32).reshape(ch * lats, M_WIN)
     for l in range(lats):
-        z_send[l // SUB, l % SUB] = f_rows[pl.ds(l, ch, stride=lats), :].astype(jnp.bfloat16)
-    z_recv[z] = z_send[z]
+        rows = f_rows[pl.ds(l, ch, stride=lats), :].astype(jnp.bfloat16)
+        for w in range(2):
+            z_send[w, l // SUB, l % SUB] = rows[w * part_ch : (w + 1) * part_ch]
+    z_recv[:, z] = z_send[:, z]
 
     pl.semaphore_wait(barrier, count)
 
     far_first = [r for k in range(n // 2, 0, -1) for r in sorted({k, n - k})]
     z_far_first = [r for k in range(nz // 2, 0, -1) for r in sorted({k, nz - k})]
-    for r in z_far_first:
-        t = wrap(z + r, nz)
-        remote(z_send.at[t], z_recv.at[z], zs_sem, zr_sem, (x, y, t, c)).start()
+    for w in range(2):
+        for r in z_far_first:
+            t = wrap(z + r, nz)
+            remote(z_send.at[w, t], z_recv.at[w, z], zs_sem.at[w], zr_sem.at[w], (x, y, t, c)).start()
 
     pair_row_load.wait()
     row_i = lax.broadcasted_iota(jnp.int32, (pairs, pairs), 0)
@@ -166,21 +168,24 @@
 
     for load in (q1_load, w_load, pair_load, q2_load):
         load.wait()
-    for g in EARLY:
+    forward(0)
+
+    def send_waves(w):
+        if nz > 1:
+            got = z_recv.at[w, 0 : nz - 1]
+            remote(got, got, zs_sem.at[w], zr_sem.at[w], (x, y, z, c)).wait_recv()
+        for l in range(SUB):
+            block = z_recv[w, :, l].reshape(nz * part_ch, M_WIN)
+            both = jnp.concatenate([nt(low_sel, block), nt(high_sel, block)], axis=1)
+            p1s[chunks + w, :, l] = (both * w_smem[SUB * z + l]).astype(jnp.bfloat16).reshape(n, n, LANE)
+        send_first(WAVE_GROUPS[w])
+
+    send_waves(0)
+    send_waves(1)
+    for g in TABLE_GROUPS[1:]:
         forward(g)
-
-    if nz > 1:
-        got = z_recv.at[0 : nz - 1]
-        remote(got, got, zs_sem, zr_sem, (x, y, z, c)).wait_recv()
-    for l in range(SUB):
-        block = z_recv[:, l].reshape(nz * ch, M_WIN)
-        weight = w_smem[SUB * z + l]
-        p1s[chunks, :, l] = (nt(low_sel, block) * weight).astype(jnp.bfloat16).reshape(n, n, LANE)
-        p1s[chunks + 1, :, l] = (nt(high_sel, block) * weight).astype(jnp.bfloat16).reshape(n, n, LANE)
-    send_first(WAVE_GROUP)
-    for g in LATE:
-        forward(g)
-    forward(WAVE_GROUP)
+    forward(WAVE_GROUPS[0])
+    forward(WAVE_GROUPS[1])
 
     swaps = []
     for g in TABLE_GROUPS:
@@ -195,48 +200,77 @@
             rows = t_sib[j].reshape(rows_of, LANE)
             t_perm[j] = jnp.dot(q2[...], rows, preferred_element_type=jnp.float32).astype(jnp.bfloat16)
 
-    received_second(WAVE_GROUP)
-    waves = jnp.concatenate([p2r[chunks + i].reshape(rows_of, LANE) for i in range(2)], axis=1)
     limit = TRUNC - SPACING * pair_smem[x * n + y] - SPACING // 2
-    for j in range(0, 2 * chunks, 2):
-        blocks = [p2r[i].reshape(rows_of, LANE) if i < chunks else t_perm[i - chunks] for i in (j, j + 1)]
-        table = jnp.concatenate(blocks, axis=1)
-        both = lax.dot_general(waves, table, (((0,), (0,)), ((), ())), preferred_element_type=jnp.float32)
-        for i in range(2):
-            first = c * half + (j + i) * LANE if j + i < chunks else other * half + (j + i - chunks) * LANE
-            column = first + lax.broadcasted_iota(jnp.int32, (LANE, LANE), 1)
-            at = i * LANE
-            sums = jnp.where(column < limit, both[:LANE, at : at + LANE], both[LANE:, at : at + LANE])
-            part[:, :, (j + i) * LANE : (j + i + 1) * LANE] = sums.reshape(nz, ch, LANE)
+
+    def product(w):
+        received_second(WAVE_GROUPS[w])
+        waves = p2r[chunks + w].reshape(rows_of, LANE)
+        low = LANE // 2
+        for j in range(0, 2 * chunks, 2):
+            blocks = [p2r[i].reshape(rows_of, LANE) if i < chunks else t_perm[i - chunks] for i in (j, j + 1)]
+            table = jnp.concatenate(blocks, axis=1)
+            both = lax.dot_general(waves, table, (((0,), (0,)), ((), ())), preferred_element_type=jnp.float32)
+            for i in range(2):
+                first = c * half + (j + i) * LANE if j + i < chunks else other * half + (j + i - chunks) * LANE
+                column = first + lax.broadcasted_iota(jnp.int32, (low, LANE), 1)
+                at = i * LANE
+                sums = jnp.where(column < limit, both[:low, at : at + LANE], both[low:, at : at + LANE])
+                part[w, :, :, (j + i) * LANE : (j + i + 1) * LANE] = sums.reshape(nz, part_ch, LANE)
 
     def up(k):
         return wrap(z + k + nz, nz)
 
     ways = ((0, 1), (1, -1)) if nz > 1 else ()
-    sends = []
-    for i, sign in ways:
-        sends.append(remote(part.at[up(3 * sign)], a3.at[i], a_ssem.at[i], a_rsem.at[i], (x, y, up(sign), c)))
-        sends.append(remote(
-            part.at[up(4), :, i * half : (i + 1) * half], a4.at[i], a_ssem.at[2 + i], a_rsem.at[2 + i],
-            (x, y, up(2 * sign), c),
-        ))
-    for i, sign in ways:
-        sends.append(remote(part.at[up(sign)], fin.at[i], f_ssem.at[i], f_rsem.at[i], (x, y, up(sign), c)))
-    for send in sends:
-        send.start()
-    for i, sign in ways:
-        sends[2 * i].wait_recv()
-        merged[i] = part[up(2 * sign)] + a3[i]
-        sends[2 * i + 1].wait_recv()
-        merged[i, :, i * half : (i + 1) * half] = merged[i, :, i * half : (i + 1) * half] + a4[i]
-        send = remote(merged.at[i], fin.at[2 + i], f_ssem.at[2 + i], f_rsem.at[2 + i], (x, y, up(2 * sign), c))
-        send.start()
-        sends.append(send)
-    total = part[z]
-    for send in sends[4:]:
-        send.wait_recv()
-    for i in range(4 if nz > 1 else 0):
-        total = total + fin[i]
+
+    def send_part(w):
+        sends = []
+        for i, sign in ways:
+            sends.append(remote(
+                part.at[w, up(3 * sign)], a3.at[w, i], a_ssem.at[w, i], a_rsem.at[w, i], (x, y, up(sign), c)
+            ))
+            sends.append(remote(
+                part.at[w, up(4), :, i * half : (i + 1) * half], a4.at[w, i], a_ssem.at[w, 2 + i],
+                a_rsem.at[w, 2 + i], (x, y, up(2 * sign), c),
+            ))
+        for i, sign in ways:
+            sends.append(remote(
+                part.at[w, up(sign)], fin.at[w, i], f_ssem.at[w, i], f_rsem.at[w, i], (x, y, up(sign), c)
+            ))
+        for send in sends:
+            send.start()
+        return sends
+
+    def merge(w, sends):
+        for i, sign in ways:
+            sends[2 * i].wait_recv()
+            merged[w, i] = part[w, up(2 * sign)] + a3[w, i]
+            sends[2 * i + 1].wait_recv()
+            at = slice(i * half, (i + 1) * half)
+            merged[w, i, :, at] = merged[w, i, :, at] + a4[w, i]
+            send = remote(
+                merged.at[w, i], fin.at[w, 2 + i], f_ssem.at[w, 2 + i], f_rsem.at[w, 2 + i], (x, y, up(2 * sign), c)
+            )
+            send.start()
+            sends.append(send)
+
+    def final(w, sends):
+        total = part[w, z]
+        for send in sends[4:]:
+            send.wait_recv()
+        for i in range(4 if nz > 1 else 0):
+            total = total + fin[w, i]
+        return total
+
+    product(0)
+    sends0 = send_part(0)
+    product(1)
+    sends1 = send_part(1)
+    merge(0, sends0)
+    merge(1, sends1)
+    total0 = final(0, sends0)
+    total1 = final(1, sends1)
+    total = jnp.concatenate([total0, total1], axis=0)
+    sends = sends0 + sends1
 
     levels = nz * 2 * ch // 2
     channel = (z * 2 + c) * ch + lax.broadcasted_iota(jnp.int32, (ch, LANE), 0)
@@ -271,16 +305,18 @@
     out_copy = pltpu.make_async_copy(out_buf, out_hbm, load_sem.at[7])
     out_copy.start()
     tile = added(e0, nz * 2, 0)
-    share(e1, y, tile, 1, [(x, wrap(y + r, n), z, c) for r in far_first])
-    tile = added(e1, n, 1)
-    share(e2, x, tile, 2, [(wrap(x + r, n), y, z, c) for r in far_first])
-    tile = added(e2, n, 2)
+    tile = jnp.sum(tile, axis=0, keepdims=True)
+    ring = [min(r, n - r) for r in range(n)]
+    steps = sorted(((i, j) for i in range(n) for j in range(n) if i or j), key=lambda s: -ring[s[0]] - ring[s[1]])
+    share(e1, x * n + y, tile, 1, [(wrap(x + i, n), wrap(y + j, n), z, c) for i, j in steps])
+    tile = added(e1, pairs, 1)
     energy_ref[0, 0] = jnp.sum(tile) / (pairs * 2 * levels * 2 * half)
 
     out_copy.wait()
     if nz > 1:
-        gone = z_send.at[0 : nz - 1]
-        remote(gone, gone, zs_sem, zr_sem, (x, y, z, c)).wait_send()
+        for w in range(2):
+            gone = z_send.at[w, 0 : nz - 1]
+            remote(gone, gone, zs_sem.at[w], zr_sem.at[w], (x, y, z, c)).wait_send()
     if n > 1:
         for g, (j0, j1) in enumerate(GROUPS):
             gone = p1s.at[j0:j1, 0 : n - 1]
@@ -289,7 +325,7 @@
             remote(gone, gone, p2s_sem.at[g], p2r_sem.at[g], (x, y, z, c)).wait_send()
     for send in swaps + sends:
         send.wait_send()
-    for sem, ref, size in ((0, e0, nz * 2), (1, e1, n), (2, e2, n)):
+    for sem, ref, size in ((0, e0, nz * 2), (1, e1, pairs)):
         if size > 1:
             gone = ref.at[0 : size - 1]
             remote(gone, gone, e_ssem.at[sem], e_rsem.at[sem], (x, y, z, c)).wait_send()
@@ -325,38 +361,37 @@
             pltpu.SMEM((lats,), f32),
             vmem((rows, rows), bf16),
             vmem((rows, rows), bf16),
-            vmem((nz, SUB, ch, M_WIN), bf16),
-            vmem((nz, SUB, ch, M_WIN), bf16),
+            vmem((2, nz, SUB, ch // 2, M_WIN), bf16),
+            vmem((2, nz, SUB, ch // 2, M_WIN), bf16),
             vmem(exchange, bf16),
             vmem(exchange, bf16),
             vmem(exchange, bf16),
             vmem(exchange, bf16),
             vmem((chunks, *exchange[1:]), bf16),
             vmem((chunks, rows, LANE), bf16),
-            vmem((nz, ch, length), f32),
-            vmem((2, ch, length), f32),
-            vmem((2, ch, half), f32),
-            vmem((2, ch, length), f32),
-            vmem((4, ch, length), f32),
+            vmem((2, nz, ch // 2, length), f32),
+            vmem((2, 2, ch // 2, length), f32),
+            vmem((2, 2, ch // 2, half), f32),
+            vmem((2, 2, ch // 2, length), f32),
+            vmem((2, 4, ch // 2, length), f32),
             vmem((ch, length), f32),
             vmem((nz * 2, 8, LANE), f32),
-            vmem((n, 8, LANE), f32),
-            vmem((n, 8, LANE), f32),
+            vmem((n * n, 1, LANE), f32),
             dma((8,)),
-            dma,
-            dma,
-            dma((groups,)),
-            dma((groups,)),
-            dma((groups,)),
-            dma((groups,)),
-            dma((groups,)),
-            dma((groups,)),
-            dma((4,)),
-            dma((4,)),
-            dma((4,)),
-            dma((4,)),
-            dma((3,)),
-            dma((3,)),
+            dma((2,)),
+            dma((2,)),
+            dma((groups,)),
+            dma((groups,)),
+            dma((groups,)),
+            dma((groups,)),
+            dma((groups,)),
+            dma((groups,)),
+            dma((2, 4)),
+            dma((2, 4)),
+            dma((2, 4)),
+            dma((2, 4)),
+            dma((2,)),
+            dma((2,)),
         ],
         compiler_params=pltpu.CompilerParams(
             collective_id=0, has_side_effects=True, vmem_limit_bytes=67_043_328

time: 72.1 us -> 70.7 us (0.981)
  Pallas kernels: 67.7 us -> 66.6 us
    pallas_call x1, Pallas kernels: 67.7 us -> 66.6 us  [shards(): pl.pallas_call(functools.partial(kernel, n, nz), out_shape=(jax.ShapeDtyp...]
where the time goes in v3:
time: 70.7 us; the launch traced here: 70.5 us
  Pallas kernels  66.6 us (94%)
  between operations  2.33 us (3%)
  local copies, waits for them, and re-layouts  1.53 us (2%)
    pallas_call x1, Pallas kernels, shards(): pl.pallas_call(functools.partial(kernel, n, nz), out_shape=(jax.ShapeDtyp...  66.6 us
    unnamed x1, local copies, waits for them, and re-layouts  1.53 us

profile of v3, /device:TPU:1, one launch (start us, length us, event | category | flops | bytes accessed | tf_op | source)
XLA Modules:
  0.0 70.5 jit_solution(4613456859417564616)
XLA Ops:
  0.6 66.6 %legendre.1 = (f32[16,1280]{1,0:T(8,128)}, f32[1,1]{1,0:T(1,128)}) custom-call(bf16[16,40,128]{2,1,0:T(8,128)(2,1)} %f_hbm.1, f32[40]{0:T(128)} %w_hbm.1, bf16[40,64,1280]{2,1,0:T(8,128)(2,1)} %leg_hbm.1, s32[1,64]{1,0:T(1,128)} %bitcast.4, s32[64]{0:T(128)} %pair_hbm.1, bf16[320,320]{1,0:T(8,128)(2,1)} %constant.4.clone.q1_hbm, ...), custom_call_target="tpu_custom_call" | custom-call | tf_op jit(solution)/shard_map/legendre/pallas_call | solution.py:347
  67.3 1.5 %copy.10 = f32[1,16,1280]{2,1,0:T(8,128)} copy(f32[1,16,1280]{2,1,0:T(8,128)} %bitcast.3) | data formatting | bytes 163840

commit v4 on v0

v4 whole, which is shorter than its diff:
```python
import functools

import jax
import jax.numpy as jnp
from jax import lax
from jax.experimental import pallas as pl
from jax.experimental.pallas import tpu as pltpu
from jax.sharding import Mesh
from jax.sharding import PartitionSpec as P

MESH = pl.DeviceIdType.MESH
TRUNC = 1280
M_WIN = 128
SPACING = 10
LAT = ("lat_0", "lat_1")
LEV = ("lev_0", "lev_1")
LANE = 128
PIECES = ((0, 3), (3, 5))


def nt(a, b):
    return lax.dot_general(a, b, (((1,), (1,)), ((), ())), preferred_element_type=jnp.float32)


def tn(a, b):
    return lax.dot_general(a, b, (((0,), (0,)), ((), ())), preferred_element_type=jnp.float32)


def one_hot(condition):
    return jnp.where(condition, 1.0, 0.0).astype(jnp.bfloat16)


def iota(shape, dim):
    return lax.broadcasted_iota(jnp.int32, shape, dim)


def lanes_for_rows(tiles, rows, width):
    row, lane = iota(tiles.shape, 1), iota(tiles.shape, 2)
    group = lax.div(lane, width)
    step = 1
    while step < rows:
        row_bit, group_bit = lax.rem(lax.div(row, step), 2), lax.rem(lax.div(group, step), 2)
        down = pltpu.roll(pltpu.roll(tiles, step, 1), LANE - step * width, 2)
        up = pltpu.roll(pltpu.roll(tiles, rows - step, 1), step * width, 2)
        moved = jnp.where(row_bit > group_bit, down, up)
        tiles = jnp.where(row_bit == group_bit, tiles, moved)
        step *= 2
    return tiles


def kernel(n, f_hbm, w_hbm, leg_hbm, pair_row_hbm, pair_hbm, out_hbm, energy_ref,
           f_in, f_rows, g, tin, pair_row, pair_smem, w_smem, z_send, z_recv, w_send, w_recv, t_send, t_recv,
           part, a3, a4, merged, fin, total_ref, e0, e1,
           load_sem, zs_sem, zr_sem, ws_sem, wr_sem, ts_sem, tr_sem,
           a_ssem, a_rsem, f_ssem, f_rsem, o_ssem, o_rsem, e_ssem, e_rsem):
    x, y, z, c = (lax.axis_index(a) for a in LAT + LEV)
    ch, lats, _ = f_in.shape
    half = tin.shape[2]
    chunks = half // LANE
    other = 1 - c
    pairs = n * n
    sources = 2 * n
    width = ch
    rows = LANE // width
    blocks = lats // rows
    sides = sources // rows
    me = z * 2 + c

    def first_axis(j):
        return (jnp.where(c == 0, j, x), jnp.where(c == 0, y, j), z, c)

    def second_axis(j):
        return (jnp.where(c == 0, x, j), jnp.where(c == 0, j, y), z, c)

    me_first = jnp.where(c == 0, x, y)
    me_second = jnp.where(c == 0, y, x)

    def wrap(v):
        return lax.rem(v + n, n)

    loads = [
        pltpu.make_async_copy(f_hbm, f_in, load_sem.at[0]),
        pltpu.make_async_copy(pair_row_hbm, pair_row, load_sem.at[1]),
        pltpu.make_async_copy(w_hbm, w_smem, load_sem.at[2]),
        pltpu.make_async_copy(leg_hbm.at[:, :, pl.ds(pl.multiple_of(c * half, LANE), half)], tin, load_sem.at[3]),
        pltpu.make_async_copy(pair_hbm, pair_smem, load_sem.at[4]),
    ]
    for load in loads:
        load.start()
    f_load, pair_row_load, w_load, table_load, pair_load = loads

    barrier = pltpu.get_barrier_semaphore()
    count = 0
    far_first = [r for k in range(n // 2, 0, -1) for r in sorted({k, n - k})]
    for r in far_first:
        for device in (
            (wrap(x + r), y, z, c), (x, wrap(y + r), z, c), (x, y, wrap(z + r), c), (x, y, wrap(z + r), other)
        ):
            pl.semaphore_signal(barrier, inc=1, device_id=device, device_id_type=MESH)
            count += 1
    pl.semaphore_signal(barrier, inc=1, device_id=(x, y, z, other), device_id_type=MESH)
    count += 1

    def remote(src, dst, ssem, rsem, device):
        return pltpu.make_async_remote_copy(
            src_ref=src, dst_ref=dst, send_sem=ssem, recv_sem=rsem, device_id=device, device_id_type=MESH
        )

    f_load.wait()
    f_rows[...] = f_in[...].astype(jnp.float32).reshape(ch * lats, M_WIN)
    for l in range(lats):
        g[l // rows, l % rows * ch : (l % rows + 1) * ch] = f_rows[pl.ds(l, ch, stride=lats), :].astype(jnp.bfloat16)

    pair_row_load.wait()
    row_i, col_i = iota((pairs, pairs), 0), iota((pairs, pairs), 1)
    swapped = one_hot(row_i == lax.rem(col_i, n) * n + lax.div(col_i, n))
    wave_i = iota((M_WIN, pairs), 0)
    ids = jnp.broadcast_to(pair_row[...], (M_WIN, pairs))
    low_hot = one_hot(wave_i == ids)
    high_hot = one_hot(M_WIN - 1 - wave_i == ids)
    plain = one_hot(row_i == col_i)
    sel = jnp.concatenate([nt(swapped, low_hot), nt(plain, low_hot), nt(plain, high_hot)], axis=0).astype(jnp.bfloat16)
    for b in range(blocks):
        got = nt(sel, g[b]).astype(jnp.bfloat16)
        z_send[:, :, b] = got.reshape(3, n, n, LANE)
    z_recv[0, me] = z_send[c, z]
    z_recv[1, me] = z_send[2, z]

    pl.semaphore_wait(barrier, count)

    def z_copy(kind, u, t, core):
        remote(z_send.at[kind, t], z_recv.at[u, me], zs_sem.at[u], zr_sem.at[u], (x, y, t, core)).start()

    for core in (1, 0):
        for r in far_first:
            z_copy(core, 0, wrap(z + r), core)
    z_copy(other, 0, z, other)
    for r in far_first:
        z_copy(2, 1, wrap(z + r), 1)

    @pl.when(c == 0)
    def _():
        z_copy(2, 1, z, 1)

    table_rows = n * rows
    device_i = lax.div(iota((table_rows, pairs), 0), rows)
    owner_i = jnp.where(c == 0, device_i * n + z, z * n + device_i)
    owner_of_row = one_hot(iota((table_rows, pairs), 1) == owner_i)
    depth = rows * pairs
    pair_of = lax.rem(iota((depth, pairs), 0), pairs)
    table_hot = one_hot(pair_of == jnp.broadcast_to(pair_row[...], (depth, pairs)))
    same_lat = lax.rem(iota((table_rows, depth), 0), rows) == lax.div(iota((table_rows, depth), 1), pairs)
    pick = jnp.where(same_lat, nt(owner_of_row, table_hot), 0.0).astype(jnp.bfloat16)
    table_load.wait()
    for b in range(blocks):
        block = tin[b * rows : (b + 1) * rows].reshape(depth, half)
        got = jnp.dot(pick, block, preferred_element_type=jnp.float32).astype(jnp.bfloat16)
        t_send[:, b] = got.reshape(n, rows, half)
    t_recv[me_first] = t_send[me_first]
    for r in far_first:
        t = wrap(me_first + r)
        remote(t_send.at[t], t_recv.at[me_first], ts_sem, tr_sem, first_axis(t)).start()

    w_load.wait()
    pair_load.wait()
    weight_row = iota((rows, LANE), 0)
    weights = []
    for b in range(blocks):
        weight = jnp.zeros((rows, LANE), jnp.float32)
        for l in range(rows):
            weight = jnp.where(weight_row == l, w_smem[b * rows + l], weight)
        weights.append(weight)
    side = sources * n
    order_i = iota((side, side), 0)
    by_device = one_hot(iota((side, side), 1) == lax.rem(order_i, sources) * n + lax.div(order_i, sources))

    def send_waves(u):
        got = z_recv.at[u, 0 : sources - 1]
        remote(got, got, zs_sem.at[u], zr_sem.at[u], (x, y, z, c)).wait_recv()
        for b in range(blocks):
            tiles = jnp.dot(by_device, z_recv[u, :, b].reshape(side, LANE), preferred_element_type=jnp.float32)
            tiles = lanes_for_rows(tiles.reshape(n * sides, rows, LANE), rows, width)
            w_send[u, :, :, b] = (tiles * weights[b][None]).astype(jnp.bfloat16).reshape(n, sides, rows, LANE)
        w_recv[u, me_first] = w_send[u, me_first]
        for r in far_first:
            t = wrap(me_first + r)
            remote(w_send.at[u, t], w_recv.at[u, me_first], ws_sem.at[u], wr_sem.at[u], first_axis(t)).start()

    def wait_waves(u):
        got = w_recv.at[u, 0 : n - 1]
        remote(got, got, ws_sem.at[u], wr_sem.at[u], (x, y, z, c)).wait_recv()

    send_waves(0)

    @pl.when(c == 1)
    def _():
        send_waves(1)

    got = t_recv.at[0 : n - 1]
    remote(got, got, ts_sem, tr_sem, (x, y, z, c)).wait_recv()
    wait_waves(0)

    @pl.when(c == 1)
    def _():
        wait_waves(1)

    depth_all = n * lats
    pair_id = pair_smem[jnp.where(c == 0, x * n + z, z * n + y)]
    limit = TRUNC - SPACING * pair_id - SPACING // 2

    def waves_of(u):
        return jnp.concatenate([w_recv[u, :, s].reshape(depth_all, LANE) for s in range(sides)], axis=1)

    def table_of(j0, j1):
        return t_recv[:, :, :, j0 * LANE : j1 * LANE].reshape(depth_all, (j1 - j0) * LANE)

    low_waves = waves_of(0)

    def product(j0, j1):
        spans = [(j, min(j + 2, j1)) for j in range(j0, j1, 2)]

        @pl.when(c == 0)
        def _():
            for k0, k1 in spans:
                sums = tn(low_waves, table_of(k0, k1))
                part[:, :, k0 * LANE : k1 * LANE] = sums.reshape(n, 2 * ch, (k1 - k0) * LANE)

        @pl.when(c == 1)
        def _():
            high_waves = waves_of(1)
            for k0, k1 in spans:
                table = table_of(k0, k1)
                column = half + k0 * LANE + iota((sources * ch, (k1 - k0) * LANE), 1)
                sums = jnp.where(column < limit, tn(low_waves, table), tn(high_waves, table))
                part[:, :, k0 * LANE : k1 * LANE] = sums.reshape(n, 2 * ch, (k1 - k0) * LANE)

    def up(k):
        return wrap(me_second + k)

    far = n == 8
    ways = ((1, -1), (0, 1)) if far else ((0, 1),)
    stage, near, late = {}, {}, {}

    def span_of(p):
        return slice(PIECES[p][0] * LANE, PIECES[p][1] * LANE)

    def send_far(p):
        at = span_of(p)
        for i, sign in ways if far else ():
            stage[p, i] = (
                remote(
                    part.at[up(3 * sign), :, at], a3.at[i, :, at], a_ssem.at[p, i], a_rsem.at[p, i],
                    second_axis(up(sign)),
                ),
                remote(
                    part.at[up(4), i * ch : (i + 1) * ch, at], a4.at[i, :, at], a_ssem.at[p, 2 + i],
                    a_rsem.at[p, 2 + i], second_axis(up(2 * sign)),
                ),
            )
            for send in stage[p, i]:
                send.start()

    def send_near(p):
        at = span_of(p)
        for i, sign in ways:
            near[p, i] = remote(
                part.at[up(sign), :, at], fin.at[i, :, at], f_ssem.at[p, i], f_rsem.at[p, i], second_axis(up(sign))
            )
            near[p, i].start()

    def merge(p):
        at = span_of(p)
        for i, sign in ways if far else ():
            stage[p, i][0].wait_recv()
            merged[i, :, at] = part[up(2 * sign), :, at] + a3[i, :, at]
            stage[p, i][1].wait_recv()
            mine = slice(i * ch, (i + 1) * ch)
            merged[i, mine, at] = merged[i, mine, at] + a4[i, :, at]
            late[p, i] = remote(
                merged.at[i, :, at], fin.at[2 + i, :, at], f_ssem.at[p, 2 + i], f_rsem.at[p, 2 + i],
                second_axis(up(2 * sign)),
            )
            late[p, i].start()

    def final(p):
        at = span_of(p)
        total = part[me_second, :, at]
        for i, _ in ways:
            near[p, i].wait_recv()
            total = total + fin[i, :, at]
        for i, _ in ways if far else ():
            late[p, i].wait_recv()
            total = total + fin[2 + i, :, at]
        return total

    product(*PIECES[0])
    send_far(0)
    product(*PIECES[1])
    send_far(1)
    send_near(0)
    merge(0)
    send_near(1)
    merge(1)
    total = jnp.concatenate([final(0), final(1)], axis=1)

    levels = sources * ch // 2
    channel = me_second * 2 * ch + iota((2 * ch, LANE), 0)
    factor = 1.0 + 2.0 * lax.shift_right_logical(channel, 1).astype(jnp.float32) / (levels - 1)
    squares = None
    for j in range(chunks):
        column = total[:, j * LANE : (j + 1) * LANE]
        squares = column * column if squares is None else squares + column * column
    squares = factor * squares
    tile = squares[0:8]
    for i in range(1, 2 * ch // 8):
        tile = tile + squares[i * 8 : i * 8 + 8]

    def share(ref, at, tile, sem, devices):
        ref[at] = tile
        for device in devices:
            remote(ref.at[at], ref.at[at], e_ssem.at[sem], e_rsem.at[sem], device).start()

    def added(ref, size, sem):
        got = ref.at[0 : size - 1]
        remote(got, got, e_ssem.at[sem], e_rsem.at[sem], (x, y, z, c)).wait_recv()
        tile = ref[0]
        for i in range(1, size):
            tile = tile + ref[i]
        return tile

    peers = [(x, y, wrap(z + r), k) for r in far_first for k in (c, other)] + [(x, y, z, other)]
    share(e0, me, tile, 0, peers)
    total_ref[...] = total

    tile = added(e0, sources, 0)
    tile = jnp.sum(tile, axis=0, keepdims=True)
    ring = [min(r, n - r) for r in range(n)]
    steps = sorted(((i, j) for i in range(n) for j in range(n) if i or j), key=lambda s: -ring[s[0]] - ring[s[1]])
    share(e1, x * n + y, tile, 1, [(wrap(x + i), wrap(y + j), z, c) for i, j in steps])

    at_home = jnp.where(c == 0, y, x) == z

    def rows_of(core):
        return total_ref.at[pl.ds(pl.multiple_of(core * ch, 8), ch)]

    home = out_hbm.at[:, pl.ds(pl.multiple_of(c * half, LANE), half)]
    at_home_copy = pltpu.make_async_copy(rows_of(c), home, load_sem.at[5])

    def to_owner(core):
        device = (jnp.where(c == 0, x, z), jnp.where(c == 0, z, y), me_second, core)
        return remote(rows_of(core), home, o_ssem.at[core], o_rsem.at[c], device)

    to_owner(other).start()

    @pl.when(at_home)
    def _():
        at_home_copy.start()

    @pl.when(jnp.logical_not(at_home))
    def _():
        to_owner(c).start()

    tile = added(e1, pairs, 1)
    energy_ref[0, 0] = jnp.sum(tile) / (pairs * 2 * levels * 2 * half)

    def from_core(core):
        got = out_hbm.at[:, pl.ds(pl.multiple_of(core * half, LANE), half)]
        return remote(got, got, o_ssem.at[core], o_rsem.at[core], (x, y, z, c))

    from_core(other).wait_recv()

    @pl.when(at_home)
    def _():
        at_home_copy.wait()

    @pl.when(jnp.logical_not(at_home))
    def _():
        from_core(c).wait_recv()

    first = z_recv.at[0, 0 : sources - 1]
    remote(first, first, zs_sem.at[0], zr_sem.at[0], (x, y, z, c)).wait_send()

    @pl.when(c == 0)
    def _():
        second = z_recv.at[1, 0:n]
        remote(second, second, zs_sem.at[1], zr_sem.at[1], (x, y, z, c)).wait_send()

    @pl.when(c == 1)
    def _():
        second = z_recv.at[1, 0 : n - 1]
        remote(second, second, zs_sem.at[1], zr_sem.at[1], (x, y, z, c)).wait_send()
        gone = w_send.at[1, 0 : n - 1]
        remote(gone, gone, ws_sem.at[1], wr_sem.at[1], (x, y, z, c)).wait_send()

    gone = w_send.at[0, 0 : n - 1]
    remote(gone, gone, ws_sem.at[0], wr_sem.at[0], (x, y, z, c)).wait_send()
    gone = t_send.at[0 : n - 1]
    remote(gone, gone, ts_sem, tr_sem, (x, y, z, c)).wait_send()
    for key in near:
        near[key].wait_send()
    for key in late:
        stage[key][0].wait_send()
        stage[key][1].wait_send()
        late[key].wait_send()
    to_owner(other).wait_send()

    @pl.when(jnp.logical_not(at_home))
    def _():
        to_owner(c).wait_send()

    for sem, ref, size in ((0, e0, sources), (1, e1, pairs)):
        gone = ref.at[0 : size - 1]
        remote(gone, gone, e_ssem.at[sem], e_rsem.at[sem], (x, y, z, c)).wait_send()


def shards(n, fourier, quad_weights, legendre, owner_pair):
    ch, lats, _ = fourier.shape
    _, pairs, length = legendre.shape
    half = length // 2
    rows = LANE // ch
    blocks = lats // rows
    sides = 2 * n // rows
    bf16, f32 = jnp.bfloat16, jnp.float32
    vmem, dma = pltpu.VMEM, pltpu.SemaphoreType.DMA
    hbm = pl.BlockSpec(memory_space=pltpu.HBM)
    smem = pl.BlockSpec(memory_space=pltpu.SMEM)
    spectra, energy = pl.pallas_call(
        functools.partial(kernel, n),
        out_shape=(
            jax.ShapeDtypeStruct((ch, length), f32),
            jax.ShapeDtypeStruct((1, 1), f32),
        ),
        in_specs=[hbm] * 5,
        out_specs=(hbm, smem),
        scratch_shapes=[
            vmem((ch, lats, M_WIN), bf16),
            vmem((ch * lats, M_WIN), f32),
            vmem((blocks, LANE, M_WIN), bf16),
            vmem((lats, pairs, half), bf16),
            vmem((1, pairs), jnp.int32),
            pltpu.SMEM((pairs,), jnp.int32),
            pltpu.SMEM((lats,), f32),
            vmem((3, n, blocks, n, LANE), bf16),
            vmem((2, 2 * n, blocks, n, LANE), bf16),
            vmem((2, n, sides, blocks, rows, LANE), bf16),
            vmem((2, n, sides, blocks, rows, LANE), bf16),
            vmem((n, blocks, rows, half), bf16),
            vmem((n, blocks, rows, half), bf16),
            vmem((n, 2 * ch, half), f32),
            vmem((2, 2 * ch, half), f32),
            vmem((2, ch, half), f32),
            vmem((2, 2 * ch, half), f32),
            vmem((4, 2 * ch, half), f32),
            vmem((2 * ch, half), f32),
            vmem((2 * n, 8, LANE), f32),
            vmem((n * n, 1, LANE), f32),
            dma((6,)),
            dma((2,)),
            dma((2,)),
            dma((2,)),
            dma((2,)),
            dma,
            dma,
            dma((2, 4)),
            dma((2, 4)),
            dma((2, 4)),
            dma((2, 4)),
            dma((2,)),
            dma((2,)),
            dma((2,)),
            dma((2,)),
        ],
        compiler_params=pltpu.CompilerParams(collective_id=0, has_side_effects=True, vmem_limit_bytes=67_043_328),
        name="legendre",
    )(fourier, quad_weights, legendre, owner_pair.reshape(1, pairs), owner_pair)
    return spectra[None], energy[0, 0]


def solution(mesh):
    n = mesh.shape["lev"] // 2
    finer = Mesh(mesh.devices.reshape(n, n, n, 2), LAT + LEV)
    return jax.shard_map(
        functools.partial(shards, n),
        mesh=finer,
        in_specs=(P(LEV, LAT, None), P(LAT), P(LAT, None, None), P()),
        out_specs=(P(LAT, LEV, None), P()),
        check_vma=False,
    )
```

time: 195 us -> 64.2 us (0.33)
  the two profiles are of different devices: /device:TPU:1 before, /device:TPU:18 now
where the time goes in v4:
time: 64.2 us; the launch traced here: 64 us
  Pallas kernels  60.2 us (94%)
  between operations  2.33 us (4%)
  local copies, waits for them, and re-layouts  1.53 us (2%)
    pallas_call x1, Pallas kernels, shards(): pl.pallas_call(functools.partial(kernel, n), out_shape=(jax.ShapeDtypeStr...  60.2 us
    unnamed x1, local copies, waits for them, and re-layouts  1.53 us

profile of v4, /device:TPU:18, one launch (start us, length us, event | category | flops | bytes accessed | tf_op | source)
XLA Modules:
  0.0 64.0 jit_solution(15644667242481006096)
XLA Ops:
  0.6 60.2 %legendre.1 = (f32[16,1280]{1,0:T(8,128)}, f32[1,1]{1,0:T(1,128)}) custom-call(bf16[16,40,128]{2,1,0:T(8,128)(2,1)} %f_hbm.1, f32[40]{0:T(128)} %w_hbm.1, bf16[40,64,1280]{2,1,0:T(8,128)(2,1)} %leg_hbm.1, s32[1,64]{1,0:T(1,128)} %bitcast.4, s32[64]{0:T(128)} %pair_hbm.1), custom_call_target="tpu_custom_call" | custom-call | tf_op jit(solution)/shard_map/legendre/pallas_call | solution.py:427
  60.8 1.5 %copy.8 = f32[1,16,1280]{2,1,0:T(8,128)} copy(f32[1,16,1280]{2,1,0:T(8,128)} %bitcast.3) | data formatting | bytes 163840

commit v5 on v4

--- a/solution.py
+++ b/solution.py
@@ -40,17 +40,18 @@
     step = 1
     while step < rows:
         row_bit, group_bit = lax.rem(lax.div(row, step), 2), lax.rem(lax.div(group, step), 2)
-        down = pltpu.roll(pltpu.roll(tiles, step, 1), LANE - step * width, 2)
-        up = pltpu.roll(pltpu.roll(tiles, rows - step, 1), step * width, 2)
-        moved = jnp.where(row_bit > group_bit, down, up)
+        moved = pltpu.roll(pltpu.roll(tiles, rows - step, 1), step * width, 2)
+        if 2 * step < rows:
+            down = pltpu.roll(pltpu.roll(tiles, step, 1), LANE - step * width, 2)
+            moved = jnp.where(row_bit > group_bit, down, moved)
         tiles = jnp.where(row_bit == group_bit, tiles, moved)
         step *= 2
     return tiles
 
 
-def kernel(n, f_hbm, w_hbm, leg_hbm, pair_row_hbm, pair_hbm, out_hbm, energy_ref,
+def kernel(n, f_hbm, w_hbm, leg_hbm, pair_row_hbm, pair_hbm, out_hbm, e1_hbm,
            f_in, f_rows, g, tin, pair_row, pair_smem, w_smem, z_send, z_recv, w_send, w_recv, t_send, t_recv,
-           part, a3, a4, merged, fin, total_ref, e0, e1,
+           part, a3, a4, merged, fin, total_ref, e0, e_row,
            load_sem, zs_sem, zr_sem, ws_sem, wr_sem, ts_sem, tr_sem,
            a_ssem, a_rsem, f_ssem, f_rsem, o_ssem, o_rsem, e_ssem, e_rsem):
     x, y, z, c = (lax.axis_index(a) for a in LAT + LEV)
@@ -131,7 +132,7 @@
     def z_copy(kind, u, t, core):
         remote(z_send.at[kind, t], z_recv.at[u, me], zs_sem.at[u], zr_sem.at[u], (x, y, t, core)).start()
 
-    for core in (1, 0):
+    for core in (0, 1):
         for r in far_first:
             z_copy(core, 0, wrap(z + r), core)
     z_copy(other, 0, z, other)
@@ -177,14 +178,20 @@
     def send_waves(u):
         got = z_recv.at[u, 0 : sources - 1]
         remote(got, got, zs_sem.at[u], zr_sem.at[u], (x, y, z, c)).wait_recv()
+        w_recv_own = w_recv.at[u, me_first]
         for b in range(blocks):
             tiles = jnp.dot(by_device, z_recv[u, :, b].reshape(side, LANE), preferred_element_type=jnp.float32)
             tiles = lanes_for_rows(tiles.reshape(n * sides, rows, LANE), rows, width)
             w_send[u, :, :, b] = (tiles * weights[b][None]).astype(jnp.bfloat16).reshape(n, sides, rows, LANE)
-        w_recv[u, me_first] = w_send[u, me_first]
-        for r in far_first:
-            t = wrap(me_first + r)
-            remote(w_send.at[u, t], w_recv.at[u, me_first], ws_sem.at[u], wr_sem.at[u], first_axis(t)).start()
+            if b + 1 not in (blocks // 2 + 1, blocks):
+                continue
+            at = slice(0, b + 1) if b + 1 < blocks else slice(blocks // 2 + 1, blocks)
+            w_recv_own[:, at] = w_send[u, me_first, :, at]
+            for r in far_first:
+                t = wrap(me_first + r)
+                remote(
+                    w_send.at[u, t, :, at], w_recv_own.at[:, at], ws_sem.at[u], wr_sem.at[u], first_axis(t)
+                ).start()
 
     def wait_waves(u):
         got = w_recv.at[u, 0 : n - 1]
@@ -200,10 +207,6 @@
     remote(got, got, ts_sem, tr_sem, (x, y, z, c)).wait_recv()
     wait_waves(0)
 
-    @pl.when(c == 1)
-    def _():
-        wait_waves(1)
-
     depth_all = n * lats
     pair_id = pair_smem[jnp.where(c == 0, x * n + z, z * n + y)]
     limit = TRUNC - SPACING * pair_id - SPACING // 2
@@ -214,25 +217,28 @@
     def table_of(j0, j1):
         return t_recv[:, :, :, j0 * LANE : j1 * LANE].reshape(depth_all, (j1 - j0) * LANE)
 
+    all_spans = [(k, min(k + 2, j1)) for j0, j1 in PIECES for k in range(j0, j1, 2)]
+
+    def sums_of(waves, k0, k1):
+        return tn(waves, table_of(k0, k1)).reshape(n, 2 * ch, (k1 - k0) * LANE)
+
     low_waves = waves_of(0)
-
-    def product(j0, j1):
-        spans = [(j, min(j + 2, j1)) for j in range(j0, j1, 2)]
-
-        @pl.when(c == 0)
-        def _():
-            for k0, k1 in spans:
-                sums = tn(low_waves, table_of(k0, k1))
-                part[:, :, k0 * LANE : k1 * LANE] = sums.reshape(n, 2 * ch, (k1 - k0) * LANE)
-
+    for k0, k1 in all_spans:
+        part[:, :, k0 * LANE : k1 * LANE] = sums_of(low_waves, k0, k1)
+
+    @pl.when(c == 1)
+    def _():
+        wait_waves(1)
+
+    def product_high(j0, j1):
         @pl.when(c == 1)
         def _():
             high_waves = waves_of(1)
-            for k0, k1 in spans:
-                table = table_of(k0, k1)
-                column = half + k0 * LANE + iota((sources * ch, (k1 - k0) * LANE), 1)
-                sums = jnp.where(column < limit, tn(low_waves, table), tn(high_waves, table))
-                part[:, :, k0 * LANE : k1 * LANE] = sums.reshape(n, 2 * ch, (k1 - k0) * LANE)
+            for k0, k1 in all_spans:
+                if j0 <= k0 < j1:
+                    at = slice(k0 * LANE, k1 * LANE)
+                    column = half + k0 * LANE + iota((n, 2 * ch, (k1 - k0) * LANE), 2)
+                    part[:, :, at] = jnp.where(column < limit, part[:, :, at], sums_of(high_waves, k0, k1))
 
     def up(k):
         return wrap(me_second + k)
@@ -293,14 +299,14 @@
             total = total + fin[2 + i, :, at]
         return total
 
-    product(*PIECES[0])
+    product_high(*PIECES[0])
     send_far(0)
-    product(*PIECES[1])
+    product_high(*PIECES[1])
     send_far(1)
     send_near(0)
     merge(0)
+    merge(1)
     send_near(1)
-    merge(1)
     total = jnp.concatenate([final(0), final(1)], axis=1)
 
     levels = sources * ch // 2
@@ -333,35 +339,41 @@
     total_ref[...] = total
 
     tile = added(e0, sources, 0)
+    at_home = jnp.where(c == 0, y, x) == z
+
+    def rows_of(core):
+        return total_ref.at[pl.ds(pl.multiple_of(core * ch, 8), ch)]
+
+    home = out_hbm.at[:, pl.ds(pl.multiple_of(c * half, LANE), half)]
+    at_home_copy = pltpu.make_async_copy(rows_of(c), home, load_sem.at[5])
+
+    def to_owner(core):
+        device = (jnp.where(c == 0, x, z), jnp.where(c == 0, z, y), me_second, core)
+        return remote(rows_of(core), home, o_ssem.at[core], o_rsem.at[c], device)
+
+    to_owner(other).start()
+
+    @pl.when(at_home)
+    def _():
+        at_home_copy.start()
+
+    @pl.when(jnp.logical_not(at_home))
+    def _():
+        to_owner(c).start()
+
     tile = jnp.sum(tile, axis=0, keepdims=True)
     ring = [min(r, n - r) for r in range(n)]
     steps = sorted(((i, j) for i in range(n) for j in range(n) if i or j), key=lambda s: -ring[s[0]] - ring[s[1]])
-    share(e1, x * n + y, tile, 1, [(wrap(x + i), wrap(y + j), z, c) for i, j in steps])
-
-    at_home = jnp.where(c == 0, y, x) == z
-
-    def rows_of(core):
-        return total_ref.at[pl.ds(pl.multiple_of(core * ch, 8), ch)]
-
-    home = out_hbm.at[:, pl.ds(pl.multiple_of(c * half, LANE), half)]
-    at_home_copy = pltpu.make_async_copy(rows_of(c), home, load_sem.at[5])
-
-    def to_owner(core):
-        device = (jnp.where(c == 0, x, z), jnp.where(c == 0, z, y), me_second, core)
-        return remote(rows_of(core), home, o_ssem.at[core], o_rsem.at[c], device)
-
-    to_owner(other).start()
-
-    @pl.when(at_home)
-    def _():
-        at_home_copy.start()
-
-    @pl.when(jnp.logical_not(at_home))
-    def _():
-        to_owner(c).start()
-
-    tile = added(e1, pairs, 1)
-    energy_ref[0, 0] = jnp.sum(tile) / (pairs * 2 * levels * 2 * half)
+    e_row[...] = tile
+    e_own = e1_hbm.at[x * n + y]
+    for i, j in steps:
+        remote(e_row, e_own, e_ssem.at[1], e_rsem.at[1], (wrap(x + i), wrap(y + j), z, c)).start()
+    e_copy = pltpu.make_async_copy(e_row, e_own, load_sem.at[6])
+    e_copy.start()
+
+    got = e1_hbm.at[0 : pairs - 1]
+    remote(got, got, e_ssem.at[1], e_rsem.at[1], (x, y, z, c)).wait_recv()
+    e_copy.wait()
 
     def from_core(core):
         got = out_hbm.at[:, pl.ds(pl.multiple_of(core * half, LANE), half)]
@@ -408,9 +420,21 @@
     def _():
         to_owner(c).wait_send()
 
-    for sem, ref, size in ((0, e0, sources), (1, e1, pairs)):
+    for sem, ref, size in ((0, e0, sources), (1, e1_hbm, pairs)):
         gone = ref.at[0 : size - 1]
         remote(gone, gone, e_ssem.at[sem], e_rsem.at[sem], (x, y, z, c)).wait_send()
+
+
+def outputs_kernel(scale, block_hbm, rows_hbm, out_hbm, energy_ref, block, rows, sem):
+    loads = [pltpu.make_async_copy(block_hbm, block, sem.at[0]), pltpu.make_async_copy(rows_hbm, rows, sem.at[1])]
+    for load in loads:
+        load.start()
+    loads[0].wait()
+    store = pltpu.make_async_copy(block, out_hbm, sem.at[2])
+    store.start()
+    loads[1].wait()
+    energy_ref[0, 0] = jnp.sum(jnp.sum(rows[...], axis=0)) * scale
+    store.wait()
 
 
 def shards(n, fourier, quad_weights, legendre, owner_pair):
@@ -424,14 +448,15 @@
     vmem, dma = pltpu.VMEM, pltpu.SemaphoreType.DMA
     hbm = pl.BlockSpec(memory_space=pltpu.HBM)
     smem = pl.BlockSpec(memory_space=pltpu.SMEM)
-    spectra, energy = pl.pallas_call(
+    limit = pltpu.CompilerParams(vmem_limit_bytes=67_043_328)
+    block, energy_rows = pl.pallas_call(
         functools.partial(kernel, n),
         out_shape=(
             jax.ShapeDtypeStruct((ch, length), f32),
-            jax.ShapeDtypeStruct((1, 1), f32),
+            jax.ShapeDtypeStruct((pairs, 1, LANE), f32),
         ),
         in_specs=[hbm] * 5,
-        out_specs=(hbm, smem),
+        out_specs=(hbm, hbm),
         scratch_shapes=[
             vmem((ch, lats, M_WIN), bf16),
             vmem((ch * lats, M_WIN), f32),
@@ -453,8 +478,8 @@
             vmem((4, 2 * ch, half), f32),
             vmem((2 * ch, half), f32),
             vmem((2 * n, 8, LANE), f32),
-            vmem((n * n, 1, LANE), f32),
-            dma((6,)),
+            vmem((1, LANE), f32),
+            dma((7,)),
             dma((2,)),
             dma((2,)),
             dma((2,)),
@@ -473,6 +498,18 @@
         compiler_params=pltpu.CompilerParams(collective_id=0, has_side_effects=True, vmem_limit_bytes=67_043_328),
         name="legendre",
     )(fourier, quad_weights, legendre, owner_pair.reshape(1, pairs), owner_pair)
+    spectra, energy = pl.pallas_call(
+        functools.partial(outputs_kernel, 1.0 / (pairs * 2 * n * ch * length)),
+        out_shape=(
+            jax.ShapeDtypeStruct((ch, length), f32),
+            jax.ShapeDtypeStruct((1, 1), f32),
+        ),
+        in_specs=[hbm] * 2,
+        out_specs=(hbm, smem),
+        scratch_shapes=[vmem((ch, length), f32), vmem((pairs, 1, LANE), f32), dma((3,))],
+        compiler_params=limit,
+        name="outputs",
+    )(block, energy_rows)
     return spectra[None], energy[0, 0]
 
 

time: 64.2 us -> 62 us (0.966)
  the two profiles are of different devices: /device:TPU:18 before, /device:TPU:1 now
where the time goes in v5:
time: 62 us; the launch traced here: 61.8 us
  Pallas kernels  61.2 us (99%)
  between operations  0.64 us (1%)
    pallas_call x1, Pallas kernels, shards(): pl.pallas_call(functools.partial(kernel, n), out_shape=(jax.ShapeDtypeStr...  59.1 us
    pallas_call x1, Pallas kernels, shards(): pl.pallas_call(functools.partial(outputs_kernel, 1.0 / (pairs * 2 * n * c...  2.06 us

profile of v5, /device:TPU:1, one launch (start us, length us, event | category | flops | bytes accessed | tf_op | source)
XLA Modules:
  0.0 61.8 jit_solution(8315478375838648810)
XLA Ops:
  0.6 59.1 %legendre.1 = (f32[16,1280]{1,0:T(8,128)}, f32[64,1,128]{2,1,0:T(1,128)}) custom-call(bf16[16,40,128]{2,1,0:T(8,128)(2,1)} %f_hbm.1, f32[40]{0:T(128)} %w_hbm.1, bf16[40,64,1280]{2,1,0:T(8,128)(2,1)} %leg_hbm.1, s32[1,64]{1,0:T(1,128)} %bitcast.3, s32[64]{0:T(128)} %pair_hbm.1), custom_call_target="tpu_custom_call" | custom-call | tf_op jit(solution)/shard_map/legendre/pallas_call | solution.py:452
  59.8 2.1 %outputs.1 = (f32[16,1280]{1,0:T(8,128)}, f32[1,1]{1,0:T(1,128)}) custom-call(f32[16,1280]{1,0:T(8,128)} %get-tuple-element.6.block_hbm, f32[64,1,128]{2,1,0:T(1,128)} %get-tuple-element.7.rows_hbm), custom_call_target="tpu_custom_call" | custom-call | tf_op jit(solution)/shard_map/outputs/pallas_call | solution.py:501

commit v6 on v5

--- a/solution.py
+++ b/solution.py
@@ -22,10 +22,6 @@
     return lax.dot_general(a, b, (((1,), (1,)), ((), ())), preferred_element_type=jnp.float32)
 
 
-def tn(a, b):
-    return lax.dot_general(a, b, (((0,), (0,)), ((), ())), preferred_element_type=jnp.float32)
-
-
 def one_hot(condition):
     return jnp.where(condition, 1.0, 0.0).astype(jnp.bfloat16)
 
@@ -34,23 +30,24 @@
     return lax.broadcasted_iota(jnp.int32, shape, dim)
 
 
-def lanes_for_rows(tiles, rows, width):
+def lanes_for_rows(tiles, paired, rows, width):
     row, lane = iota(tiles.shape, 1), iota(tiles.shape, 2)
     group = lax.div(lane, width)
     step = 1
     while step < rows:
         row_bit, group_bit = lax.rem(lax.div(row, step), 2), lax.rem(lax.div(group, step), 2)
-        moved = pltpu.roll(pltpu.roll(tiles, rows - step, 1), step * width, 2)
+        swapped_up = paired if step == 1 else pltpu.roll(tiles, rows - step, 1)
+        moved = pltpu.roll(swapped_up, step * width, 2)
         if 2 * step < rows:
-            down = pltpu.roll(pltpu.roll(tiles, step, 1), LANE - step * width, 2)
-            moved = jnp.where(row_bit > group_bit, down, moved)
+            swapped_down = paired if step == 1 else pltpu.roll(tiles, step, 1)
+            moved = jnp.where(row_bit > group_bit, pltpu.roll(swapped_down, LANE - step * width, 2), moved)
         tiles = jnp.where(row_bit == group_bit, tiles, moved)
         step *= 2
     return tiles
 
 
 def kernel(n, f_hbm, w_hbm, leg_hbm, pair_row_hbm, pair_hbm, out_hbm, e1_hbm,
-           f_in, f_rows, g, tin, pair_row, pair_smem, w_smem, z_send, z_recv, w_send, w_recv, t_send, t_recv,
+           f_in, f_rows, g, tin, pair_row, pair_smem, w_smem, z_send, z_recv, w_send, w_recv, w_turned, t_send, t_recv,
            part, a3, a4, merged, fin, total_ref, e0, e_row,
            load_sem, zs_sem, zr_sem, ws_sem, wr_sem, ts_sem, tr_sem,
            a_ssem, a_rsem, f_ssem, f_rsem, o_ssem, o_rsem, e_ssem, e_rsem):
@@ -107,11 +104,6 @@
             src_ref=src, dst_ref=dst, send_sem=ssem, recv_sem=rsem, device_id=device, device_id_type=MESH
         )
 
-    f_load.wait()
-    f_rows[...] = f_in[...].astype(jnp.float32).reshape(ch * lats, M_WIN)
-    for l in range(lats):
-        g[l // rows, l % rows * ch : (l % rows + 1) * ch] = f_rows[pl.ds(l, ch, stride=lats), :].astype(jnp.bfloat16)
-
     pair_row_load.wait()
     row_i, col_i = iota((pairs, pairs), 0), iota((pairs, pairs), 1)
     swapped = one_hot(row_i == lax.rem(col_i, n) * n + lax.div(col_i, n))
@@ -121,6 +113,11 @@
     high_hot = one_hot(M_WIN - 1 - wave_i == ids)
     plain = one_hot(row_i == col_i)
     sel = jnp.concatenate([nt(swapped, low_hot), nt(plain, low_hot), nt(plain, high_hot)], axis=0).astype(jnp.bfloat16)
+    f_load.wait()
+    f_rows[...] = f_in[...].astype(jnp.float32).reshape(ch * lats, M_WIN)
+    for l in range(lats):
+        g[l // rows, l % rows * ch : (l % rows + 1) * ch] = f_rows[pl.ds(l, ch, stride=lats), :].astype(jnp.bfloat16)
+
     for b in range(blocks):
         got = nt(sel, g[b]).astype(jnp.bfloat16)
         z_send[:, :, b] = got.reshape(3, n, n, LANE)
@@ -172,8 +169,11 @@
             weight = jnp.where(weight_row == l, w_smem[b * rows + l], weight)
         weights.append(weight)
     side = sources * n
-    order_i = iota((side, side), 0)
-    by_device = one_hot(iota((side, side), 1) == lax.rem(order_i, sources) * n + lax.div(order_i, sources))
+    order_i = iota((2 * side, side), 0)
+    source_i = lax.rem(order_i, sources)
+    paired_i = source_i + 1 - 2 * lax.rem(source_i, 2)
+    source_i = jnp.where(order_i < side, source_i, paired_i)
+    by_device = one_hot(iota((2 * side, side), 1) == source_i * n + lax.div(lax.rem(order_i, side), sources))
 
     def send_waves(u):
         got = z_recv.at[u, 0 : sources - 1]
@@ -181,7 +181,8 @@
         w_recv_own = w_recv.at[u, me_first]
         for b in range(blocks):
             tiles = jnp.dot(by_device, z_recv[u, :, b].reshape(side, LANE), preferred_element_type=jnp.float32)
-            tiles = lanes_for_rows(tiles.reshape(n * sides, rows, LANE), rows, width)
+            tiles = tiles.reshape(2, n * sides, rows, LANE)
+            tiles = lanes_for_rows(tiles[0], tiles[1], rows, width)
             w_send[u, :, :, b] = (tiles * weights[b][None]).astype(jnp.bfloat16).reshape(n, sides, rows, LANE)
             if b + 1 not in (blocks // 2 + 1, blocks):
                 continue
@@ -211,34 +212,36 @@
     pair_id = pair_smem[jnp.where(c == 0, x * n + z, z * n + y)]
     limit = TRUNC - SPACING * pair_id - SPACING // 2
 
-    def waves_of(u):
-        return jnp.concatenate([w_recv[u, :, s].reshape(depth_all, LANE) for s in range(sides)], axis=1)
+    def turn_waves(u):
+        for s in range(sides):
+            w_turned[u, s * LANE : (s + 1) * LANE] = w_recv[u, :, s].reshape(depth_all, LANE).T
 
     def table_of(j0, j1):
         return t_recv[:, :, :, j0 * LANE : j1 * LANE].reshape(depth_all, (j1 - j0) * LANE)
 
     all_spans = [(k, min(k + 2, j1)) for j0, j1 in PIECES for k in range(j0, j1, 2)]
 
-    def sums_of(waves, k0, k1):
-        return tn(waves, table_of(k0, k1)).reshape(n, 2 * ch, (k1 - k0) * LANE)
-
-    low_waves = waves_of(0)
+    def sums_of(u, k0, k1):
+        sums = jnp.dot(w_turned[u], table_of(k0, k1), preferred_element_type=jnp.float32)
+        return sums.reshape(n, 2 * ch, (k1 - k0) * LANE)
+
+    turn_waves(0)
     for k0, k1 in all_spans:
-        part[:, :, k0 * LANE : k1 * LANE] = sums_of(low_waves, k0, k1)
+        part[:, :, k0 * LANE : k1 * LANE] = sums_of(0, k0, k1)
 
     @pl.when(c == 1)
     def _():
         wait_waves(1)
+        turn_waves(1)
 
     def product_high(j0, j1):
         @pl.when(c == 1)
         def _():
-            high_waves = waves_of(1)
             for k0, k1 in all_spans:
                 if j0 <= k0 < j1:
                     at = slice(k0 * LANE, k1 * LANE)
                     column = half + k0 * LANE + iota((n, 2 * ch, (k1 - k0) * LANE), 2)
-                    part[:, :, at] = jnp.where(column < limit, part[:, :, at], sums_of(high_waves, k0, k1))
+                    part[:, :, at] = jnp.where(column < limit, part[:, :, at], sums_of(1, k0, k1))
 
     def up(k):
         return wrap(me_second + k)
@@ -425,16 +428,18 @@
         remote(gone, gone, e_ssem.at[sem], e_rsem.at[sem], (x, y, z, c)).wait_send()
 
 
-def outputs_kernel(scale, block_hbm, rows_hbm, out_hbm, energy_ref, block, rows, sem):
-    loads = [pltpu.make_async_copy(block_hbm, block, sem.at[0]), pltpu.make_async_copy(rows_hbm, rows, sem.at[1])]
+def outputs_kernel(scale, block_hbm, rows_hbm, out_hbm, energy_hbm, block, rows, energy, sem):
+    loads = [pltpu.make_async_copy(rows_hbm, rows, sem.at[0]), pltpu.make_async_copy(block_hbm, block, sem.at[1])]
+    stores = [pltpu.make_async_copy(energy, energy_hbm, sem.at[2]), pltpu.make_async_copy(block, out_hbm, sem.at[3])]
     for load in loads:
         load.start()
+    loads[1].wait()
+    stores[1].start()
     loads[0].wait()
-    store = pltpu.make_async_copy(block, out_hbm, sem.at[2])
-    store.start()
-    loads[1].wait()
-    energy_ref[0, 0] = jnp.sum(jnp.sum(rows[...], axis=0)) * scale
-    store.wait()
+    energy[0, 0] = jnp.sum(jnp.sum(rows[...], axis=0)) * scale
+    stores[0].start()
+    for store in stores:
+        store.wait()
 
 
 def shards(n, fourier, quad_weights, legendre, owner_pair):
@@ -447,7 +452,6 @@
     bf16, f32 = jnp.bfloat16, jnp.float32
     vmem, dma = pltpu.VMEM, pltpu.SemaphoreType.DMA
     hbm = pl.BlockSpec(memory_space=pltpu.HBM)
-    smem = pl.BlockSpec(memory_space=pltpu.SMEM)
     limit = pltpu.CompilerParams(vmem_limit_bytes=67_043_328)
     block, energy_rows = pl.pallas_call(
         functools.partial(kernel, n),
@@ -469,6 +473,7 @@
             vmem((2, 2 * n, blocks, n, LANE), bf16),
             vmem((2, n, sides, blocks, rows, LANE), bf16),
             vmem((2, n, sides, blocks, rows, LANE), bf16),
+            vmem((2, 2 * n * ch, n * lats), bf16),
             vmem((n, blocks, rows, half), bf16),
             vmem((n, blocks, rows, half), bf16),
             vmem((n, 2 * ch, half), f32),
@@ -505,8 +510,8 @@
             jax.ShapeDtypeStruct((1, 1), f32),
         ),
         in_specs=[hbm] * 2,
-        out_specs=(hbm, smem),
-        scratch_shapes=[vmem((ch, length), f32), vmem((pairs, 1, LANE), f32), dma((3,))],
+        out_specs=(hbm, hbm),
+        scratch_shapes=[vmem((ch, length), f32), vmem((pairs, 1, LANE), f32), pltpu.SMEM((1, 1), f32), dma((4,))],
         compiler_params=limit,
         name="outputs",
     )(block, energy_rows)

time: 62 us -> 61.6 us (level)
  no operation moved by 1% of the time
where the time goes in v6:
time: 61.6 us; the launch traced here: 61.4 us
  Pallas kernels  60.8 us (99%)
  between operations  0.64 us (1%)
    pallas_call x1, Pallas kernels, shards(): pl.pallas_call(functools.partial(kernel, n), out_shape=(jax.ShapeDtypeStr...  59.1 us
    pallas_call x1, Pallas kernels, shards(): pl.pallas_call(functools.partial(outputs_kernel, 1.0 / (pairs * 2 * n * c...  1.65 us

profile of v6, /device:TPU:1, one launch (start us, length us, event | category | flops | bytes accessed | tf_op | source)
XLA Modules:
  0.0 61.4 jit_solution(12086045054116104686)
XLA Ops:
  0.6 59.1 %legendre.1 = (f32[16,1280]{1,0:T(8,128)}, f32[64,1,128]{2,1,0:T(1,128)}) custom-call(bf16[16,40,128]{2,1,0:T(8,128)(2,1)} %f_hbm.1, f32[40]{0:T(128)} %w_hbm.1, bf16[40,64,1280]{2,1,0:T(8,128)(2,1)} %leg_hbm.1, s32[1,64]{1,0:T(1,128)} %bitcast.3, s32[64]{0:T(128)} %pair_hbm.1), custom_call_target="tpu_custom_call" | custom-call | tf_op jit(solution)/shard_map/legendre/pallas_call | solution.py:456
  59.8 1.6 %outputs.1 = (f32[16,1280]{1,0:T(8,128)}, f32[1,1]{1,0:T(1,128)}) custom-call(f32[16,1280]{1,0:T(8,128)} %get-tuple-element.6.block_hbm, f32[64,1,128]{2,1,0:T(1,128)} %get-tuple-element.7.rows_hbm), custom_call_target="tpu_custom_call" | custom-call | tf_op jit(solution)/shard_map/outputs/pallas_call | solution.py:506

commit v7 on v6

--- a/solution.py
+++ b/solution.py
@@ -323,6 +323,7 @@
     tile = squares[0:8]
     for i in range(1, 2 * ch // 8):
         tile = tile + squares[i * 8 : i * 8 + 8]
+    tile = jnp.sum(tile, axis=0, keepdims=True)
 
     def share(ref, at, tile, sem, devices):
         ref[at] = tile
@@ -354,23 +355,27 @@
         device = (jnp.where(c == 0, x, z), jnp.where(c == 0, z, y), me_second, core)
         return remote(rows_of(core), home, o_ssem.at[core], o_rsem.at[c], device)
 
-    to_owner(other).start()
-
-    @pl.when(at_home)
-    def _():
-        at_home_copy.start()
-
-    @pl.when(jnp.logical_not(at_home))
-    def _():
-        to_owner(c).start()
-
-    tile = jnp.sum(tile, axis=0, keepdims=True)
     ring = [min(r, n - r) for r in range(n)]
     steps = sorted(((i, j) for i in range(n) for j in range(n) if i or j), key=lambda s: -ring[s[0]] - ring[s[1]])
     e_row[...] = tile
     e_own = e1_hbm.at[x * n + y]
-    for i, j in steps:
-        remote(e_row, e_own, e_ssem.at[1], e_rsem.at[1], (wrap(x + i), wrap(y + j), z, c)).start()
+    def share_row(steps):
+        for i, j in steps:
+            remote(e_row, e_own, e_ssem.at[1], e_rsem.at[1], (wrap(x + i), wrap(y + j), z, c)).start()
+
+    far_steps = len(steps) // 3
+    share_row(steps[:far_steps])
+    to_owner(other).start()
+
+    @pl.when(at_home)
+    def _():
+        at_home_copy.start()
+
+    @pl.when(jnp.logical_not(at_home))
+    def _():
+        to_owner(c).start()
+
+    share_row(steps[far_steps:])
     e_copy = pltpu.make_async_copy(e_row, e_own, load_sem.at[6])
     e_copy.start()
 
@@ -482,7 +487,7 @@
             vmem((2, 2 * ch, half), f32),
             vmem((4, 2 * ch, half), f32),
             vmem((2 * ch, half), f32),
-            vmem((2 * n, 8, LANE), f32),
+            vmem((2 * n, 1, LANE), f32),
             vmem((1, LANE), f32),
             dma((7,)),
             dma((2,)),

time: 61.6 us -> 60.8 us (0.987)
  Pallas kernels: 60.8 us -> 60 us
    pallas_call x1, Pallas kernels: 59.1 us -> 58.3 us  [shards(): pl.pallas_call(functools.partial(kernel, n), out_shape=(jax.ShapeDtypeStr...]
where the time goes in v7:
time: 60.8 us; the launch traced here: 60.6 us
  Pallas kernels  60 us (99%)
  between operations  0.64 us (1%)
    pallas_call x1, Pallas kernels, shards(): pl.pallas_call(functools.partial(kernel, n), out_shape=(jax.ShapeDtypeStr...  58.3 us
    pallas_call x1, Pallas kernels, shards(): pl.pallas_call(functools.partial(outputs_kernel, 1.0 / (pairs * 2 * n * c...  1.65 us

profile of v7, /device:TPU:1, one launch (start us, length us, event | category | flops | bytes accessed | tf_op | source)
XLA Modules:
  0.0 60.6 jit_solution(16769631655083424903)
XLA Ops:
  0.6 58.3 %legendre.1 = (f32[16,1280]{1,0:T(8,128)}, f32[64,1,128]{2,1,0:T(1,128)}) custom-call(bf16[16,40,128]{2,1,0:T(8,128)(2,1)} %f_hbm.1, f32[40]{0:T(128)} %w_hbm.1, bf16[40,64,1280]{2,1,0:T(8,128)(2,1)} %leg_hbm.1, s32[1,64]{1,0:T(1,128)} %bitcast.3, s32[64]{0:T(128)} %pair_hbm.1), custom_call_target="tpu_custom_call" | custom-call | tf_op jit(solution)/shard_map/legendre/pallas_call | solution.py:461
  59.0 1.6 %outputs.1 = (f32[16,1280]{1,0:T(8,128)}, f32[1,1]{1,0:T(1,128)}) custom-call(f32[16,1280]{1,0:T(8,128)} %get-tuple-element.6.block_hbm, f32[64,1,128]{2,1,0:T(1,128)} %get-tuple-element.7.rows_hbm), custom_call_target="tpu_custom_call" | custom-call | tf_op jit(solution)/shard_map/outputs/pallas_call | solution.py:511

commit v8 on v7

--- a/solution.py
+++ b/solution.py
@@ -92,7 +92,7 @@
     far_first = [r for k in range(n // 2, 0, -1) for r in sorted({k, n - k})]
     for r in far_first:
         for device in (
-            (wrap(x + r), y, z, c), (x, wrap(y + r), z, c), (x, y, wrap(z + r), c), (x, y, wrap(z + r), other)
+            (x, y, wrap(z + r), c), (x, y, wrap(z + r), other), (wrap(x + r), y, z, c), (x, wrap(y + r), z, c)
         ):
             pl.semaphore_signal(barrier, inc=1, device_id=device, device_id_type=MESH)
             count += 1

time: 60.8 us -> 60.7 us (level)
  no operation moved by 1% of the time
where the time goes in v8:
time: 60.7 us; the launch traced here: 60.6 us
  Pallas kernels  59.9 us (99%)
  between operations  0.64 us (1%)
    pallas_call x1, Pallas kernels, shards(): pl.pallas_call(functools.partial(kernel, n), out_shape=(jax.ShapeDtypeStr...  58.3 us
    pallas_call x1, Pallas kernels, shards(): pl.pallas_call(functools.partial(outputs_kernel, 1.0 / (pairs * 2 * n * c...  1.65 us

profile of v8, /device:TPU:1, one launch (start us, length us, event | category | flops | bytes accessed | tf_op | source)
XLA Modules:
  0.0 60.6 jit_solution(9959527109529201453)
XLA Ops:
  0.6 58.3 %legendre.1 = (f32[16,1280]{1,0:T(8,128)}, f32[64,1,128]{2,1,0:T(1,128)}) custom-call(bf16[16,40,128]{2,1,0:T(8,128)(2,1)} %f_hbm.1, f32[40]{0:T(128)} %w_hbm.1, bf16[40,64,1280]{2,1,0:T(8,128)(2,1)} %leg_hbm.1, s32[1,64]{1,0:T(1,128)} %bitcast.3, s32[64]{0:T(128)} %pair_hbm.1), custom_call_target="tpu_custom_call" | custom-call | tf_op jit(solution)/shard_map/legendre/pallas_call | solution.py:461
  58.9 1.6 %outputs.1 = (f32[16,1280]{1,0:T(8,128)}, f32[1,1]{1,0:T(1,128)}) custom-call(f32[16,1280]{1,0:T(8,128)} %get-tuple-element.6.block_hbm, f32[64,1,128]{2,1,0:T(1,128)} %get-tuple-element.7.rows_hbm), custom_call_target="tpu_custom_call" | custom-call | tf_op jit(solution)/shard_map/outputs/pallas_call | solution.py:511
